TPU v7x, 256 devices: a whole 4x4x8 slice. The times are simulated.
256 devices in a mesh: blk: 64 (over x_hi, y, z), chan: 4 (over x_lo, core).
Axes of the slice: x: 4 (x_hi: 2, x_lo: 2; x = x_hi * 2 + x_lo), y: 4, z: 8, core: 2. Of those that a mesh axis runs over, the one named last changes fastest.
Arguments:
- pair_map: int32 [128, 2], P('blk'), may hold values from 0 to 15, as said below
- visibilities: bfloat16 [2, 128, 64, 1024], P(None, 'blk', 'chan'), may hold values from -24 to 24
- model_vis: bfloat16 [2, 128, 64, 1024], P(None, 'blk', 'chan'), may hold values from -7.2 to 7.2
- flag_mask: int32 [128, 64, 1024], P('blk', 'chan'), may hold values 0 or 1
- gain_amp: float32 [512], replicated, may hold values from 0.19 to 3.17
- gain_phase: float32 [512], replicated, may hold values from -3.1416 to 3.1416
- row_index: int32 [4, 64, 64, 256], P('chan', 'blk'), may hold values from -1 to 32767, as said below
- cell_codes: int32 [2, 4, 64, 64, 256], P(None, 'chan', 'blk'), may hold values from 32 to 992
Outputs:
- grid_tiles: float32 [4, 64, 2, 128, 128], P('chan', 'blk')
- solved_gains: float32 [2, 512], replicated
Inputs may be any that keep to these rules, and one draw needn't show every extreme that they name: `pair_map`: each row is a pair (p, q) of station blocks with p <= q; no two rows are the same pair; every station block appears in some row. `row_index`: each visibility of an index of blk and a channel group appears in at most one row of that index and group; about half of the rows are -1.
All inputs are finite; a program needn't handle non-finite values. No bound on the sum of `flag_mask` on one device may be relied on, other than what follows from the above.
Results may differ from a plain program's by a relative error of at most 0.009.
Values may be sent and summed in bfloat16 or wider, within the bound.
A program may use at most 64 MiB of HBM per device.

v0:
```python
import functools
import math

import jax
import jax.numpy as jnp
from jax import lax
from jax.sharding import Mesh
from jax.sharding import PartitionSpec as P

S = 512
BS = 32
ITERS = 3
TS = 128
KS = 8
OVER = 8
BLK = ("blk_0", "blk_1", "blk_2")
BLK_CHAN = ("blk_0", "blk_1", "blk_2", "chan_0", "chan_1")
CHAN = ("chan_0", "chan_1")


def sent_together(arrays, axis, split_dim, concat_dim, along):
    both = jnp.concatenate(arrays, axis=along)
    filled, at, gathered = (
        lax.all_to_all(both, axis, split_axis=split_dim, concat_axis=concat_dim, tiled=True),
        0,
        [],
    )
    for a in arrays:
        gathered.append(lax.slice_in_dim(filled, at, at + a.shape[along], axis=along))
        at += a.shape[along]
    return tuple(gathered)


def over_axes(shard, axes):
    return functools.reduce(lax.psum, axes, shard)


def kernel_rows(code_values):
    centre = code_values.astype(jnp.float32) / OVER
    cell_axis = jnp.arange(TS, dtype=jnp.float32)
    offset = cell_axis - centre[..., None]
    inside = jnp.abs(offset) < 0.5 * KS
    return jnp.where(inside, jnp.cos(math.pi * offset / KS) ** 2, 0.0).astype(jnp.bfloat16)


def grid_piece(real_rows, imag_rows, u_values, v_values):
    kernel_u = kernel_rows(u_values)
    kernel_v = kernel_rows(v_values).astype(jnp.float32)
    weighted = jnp.stack(
        (
            kernel_v * real_rows.astype(jnp.float32)[..., None],
            kernel_v * imag_rows.astype(jnp.float32)[..., None],
        ),
        axis=-2,
    ).astype(jnp.bfloat16)
    return jnp.einsum("grx,grcy->gcxy", kernel_u, weighted, preferred_element_type=jnp.float32)


def grid_groups(real_rows, imag_rows, u_values, v_values):
    tile_count = real_rows.shape[0]
    group_size = math.gcd(tile_count, 8)

    def regroup(member):
        return member.reshape((tile_count // group_size, group_size) + member.shape[1:])

    members = (regroup(real_rows), regroup(imag_rows), regroup(u_values), regroup(v_values))

    def advance(running, pieces):
        result = grid_piece(pieces[0], pieces[1], pieces[2], pieces[3])
        return (running + jnp.sum(result, axis=0), None)

    running, stacked = lax.scan(advance, jnp.zeros((2, TS, TS), jnp.float32), members)
    return running


def contract(form, left, right):
    return jnp.einsum(form, left, right, precision=lax.Precision.HIGHEST)


def block_gains(gain_real, gain_imag, onehot_first, onehot_second):
    tables = jnp.stack((gain_real, gain_imag)).reshape(2, S // BS, BS)
    return (
        contract("kn,cns->cks", onehot_first, tables),
        contract("kn,cns->cks", onehot_second, tables),
    )


def station_terms(
    cross_real, cross_imag, model_power, gain_real, gain_imag, onehot_first, onehot_second
):
    first_gains, second_gains = block_gains(gain_real, gain_imag, onehot_first, onehot_second)
    first_real, first_imag = (first_gains[0], first_gains[1])
    second_real, second_imag = (second_gains[0], second_gains[1])
    first_terms = jnp.stack(
        (
            contract("kij,kj->ki", cross_real, second_real)
            - contract("kij,kj->ki", cross_imag, second_imag),
            contract("kij,kj->ki", cross_real, second_imag)
            + contract("kij,kj->ki", cross_imag, second_real),
            contract(
                "kij,kj->ki", model_power, second_real * second_real + second_imag * second_imag
            ),
        )
    )
    second_terms = jnp.stack(
        (
            contract("kij,ki->kj", cross_real, first_real)
            + contract("kij,ki->kj", cross_imag, first_imag),
            contract("kij,ki->kj", cross_real, first_imag)
            - contract("kij,ki->kj", cross_imag, first_real),
            contract("kij,ki->kj", model_power, first_real * first_real + first_imag * first_imag),
        )
    )
    placed = contract("kn,cks->cns", onehot_first, first_terms) + contract(
        "kn,cks->cns", onehot_second, second_terms
    )
    placed = placed.reshape(3, S)
    return (placed[0], placed[1], placed[2])


def shards(
    pair_map, visibilities, model_vis, flag_mask, gain_amp, gain_phase, row_index, cell_codes
):
    moved_u, moved_v = sent_together((cell_codes[0, 0, 0], cell_codes[1, 0, 0]), BLK, 0, 0, 1)
    slot_count = pair_map.shape[0]
    chan_count = visibilities.shape[2]
    block_count = S // BS
    baseline = jnp.arange(BS * BS, dtype=jnp.int32)
    first_block = pair_map[:, 0]
    second_block = pair_map[:, 1]
    first_station = first_block[:, None] * BS + baseline[None, :] // BS
    second_station = second_block[:, None] * BS + baseline[None, :] % BS
    weight = (
        flag_mask.astype(jnp.float32)
        * (first_station != second_station).astype(jnp.float32)[:, None, :]
    )
    weight = weight.reshape(slot_count, chan_count, BS, BS)
    square_shape = (slot_count, chan_count, BS, BS)
    vis_real = visibilities[0].astype(jnp.float32).reshape(square_shape)
    vis_imag = visibilities[1].astype(jnp.float32).reshape(square_shape)
    model_real = model_vis[0].astype(jnp.float32).reshape(square_shape)
    model_imag = model_vis[1].astype(jnp.float32).reshape(square_shape)
    cross_real = jnp.sum(weight * (vis_real * model_real + vis_imag * model_imag), axis=1)
    cross_imag = jnp.sum(weight * (vis_imag * model_real - vis_real * model_imag), axis=1)
    model_power = jnp.sum(weight * (model_real * model_real + model_imag * model_imag), axis=1)
    block_axis = jnp.arange(block_count, dtype=jnp.int32)
    onehot_first = (first_block[:, None] == block_axis[None, :]).astype(jnp.float32)
    onehot_second = (second_block[:, None] == block_axis[None, :]).astype(jnp.float32)
    gain_real = gain_amp * jnp.cos(gain_phase)
    gain_imag = gain_amp * jnp.sin(gain_phase)
    for sweep_index in range(ITERS):
        terms = station_terms(
            cross_real, cross_imag, model_power, gain_real, gain_imag, onehot_first, onehot_second
        )
        numerator_real, numerator_imag, denominator = (
            over_axes(terms[0], BLK_CHAN),
            over_axes(terms[1], BLK_CHAN),
            over_axes(terms[2], BLK_CHAN),
        )
        update_real = numerator_real / denominator
        update_imag = numerator_imag / denominator
        if sweep_index % 2 == 1:
            gain_real = 0.5 * (update_real + gain_real)
            gain_imag = 0.5 * (update_imag + gain_imag)
        else:
            gain_real = update_real
            gain_imag = update_imag
    first_gains, second_gains = block_gains(gain_real, gain_imag, onehot_first, onehot_second)
    first_real = first_gains[0][:, None, :, None]
    first_imag = first_gains[1][:, None, :, None]
    second_real = second_gains[0][:, None, None, :]
    second_imag = second_gains[1][:, None, None, :]
    twisted_real = model_real * second_real + model_imag * second_imag
    twisted_imag = model_imag * second_real - model_real * second_imag
    predicted_real = first_real * twisted_real - first_imag * twisted_imag
    predicted_imag = first_real * twisted_imag + first_imag * twisted_real
    resid_real = (weight * (vis_real - predicted_real)).astype(jnp.bfloat16).reshape(-1)
    resid_imag = (weight * (vis_imag - predicted_imag)).astype(jnp.bfloat16).reshape(-1)
    slot_rows = row_index[0, 0]
    live_rows = slot_rows >= 0
    safe_rows = jnp.where(live_rows, slot_rows, 0)
    rows_real = jnp.where(live_rows, resid_real[safe_rows], 0.0)
    rows_imag = jnp.where(live_rows, resid_imag[safe_rows], 0.0)
    got_real, got_imag = sent_together((rows_real, rows_imag), BLK, 0, 0, 1)
    owned = grid_groups(got_real, got_imag, moved_u, moved_v)[None]
    return (owned[None], jnp.stack((gain_real, gain_imag)))


def solution(mesh):
    split = Mesh(
        mesh.devices.reshape(2, 4, 8, 2, 2), ("blk_0", "blk_1", "blk_2", "chan_0", "chan_1")
    )
    placed = (
        P(BLK, None),
        P(None, BLK, CHAN, None),
        P(None, BLK, CHAN, None),
        P(BLK, CHAN, None),
        P(),
        P(),
        P(CHAN, BLK, None, None),
        P(None, CHAN, BLK, None, None),
    )
    return jax.shard_map(
        shards,
        mesh=split,
        in_specs=placed,
        out_specs=(P(CHAN, BLK, None, None, None), P()),
        check_vma=False,
    )
```

profile of v0, /device:TPU:1, one launch (start us, length us, event | category | flops | bytes accessed | tf_op | source)
XLA Modules:
  0.0 441.7 jit_solution(7800216810703512805)
XLA Ops:
  0.6 0.7 copy-done.4
  1.6 1.2 fusion.20
  2.9 0.6 copy-done.5
  6.8 5.9 %all-reduce.14 = (f32[512]{0:T(512)S(1)}, f32[512]{0:T(512)S(1)}, f32[512]{0:T(512)S(1)}) all-reduce(f32[512]{0:T(512)S(1)} %squeeze.88, f32[512]{0:T(512)S(1)} %squeeze.89, f32[512]{0:T(512)S(1)} %squeeze.90), channel_id=1, replica_groups=mesh['blk_0'=2,'blk_1'=4,'blk_2'=8,'chan_0'=2,'chan_1'=2] {'blk_0'}, use_global_device_ids=true, to_apply=%region_3.4 | all-reduce | flops 1536 | bytes 12288 | tf_op jit(solution)/shard_map/psum | solution.py:35
  12.7 9.0 %all-reduce.5 = (f32[512]{0:T(512)S(1)}, f32[512]{0:T(512)S(1)}, f32[512]{0:T(512)S(1)}) all-reduce(f32[512]{0:T(512)S(1)} %get-tuple-element.181, f32[512]{0:T(512)S(1)} %get-tuple-element.182, f32[512]{0:T(512)S(1)} %get-tuple-element.183), channel_id=1, replica_groups=mesh['blk_0'=2,'blk_1'=4,'blk_2'=8,'chan_0'=2,'chan_1'=2] {'blk_1'}, use_global_device_ids=true, to_apply=%region_4.5 | all-reduce | flops 1536 | bytes 12288 | tf_op jit(solution)/shard_map/psum | solution.py:35
  21.7 16.5 %all-reduce.2 = (f32[512]{0:T(512)S(1)}, f32[512]{0:T(512)S(1)}, f32[512]{0:T(512)S(1)}) all-reduce(f32[512]{0:T(512)S(1)} %get-tuple-element.154, f32[512]{0:T(512)S(1)} %get-tuple-element.155, f32[512]{0:T(512)S(1)} %get-tuple-element.156), channel_id=1, replica_groups=mesh['blk_0'=2,'blk_1'=4,'blk_2'=8,'chan_0'=2,'chan_1'=2] {'blk_2'}, use_global_device_ids=true, to_apply=%region_5.6 | all-reduce | flops 1536 | bytes 12288 | tf_op jit(solution)/shard_map/psum | solution.py:35
  38.2 3.8 all-reduce.11
  42.0 10.9 %all-reduce.8 = (f32[512]{0:T(512)S(1)}, f32[512]{0:T(512)S(1)}, f32[512]{0:T(512)S(1)}) all-reduce(f32[512]{0:T(512)S(1)} %get-tuple-element.172, f32[512]{0:T(512)S(1)} %get-tuple-element.173, f32[512]{0:T(512)S(1)} %get-tuple-element.174), channel_id=1, replica_groups=mesh['blk_0'=2,'blk_1'=4,'blk_2'=8,'chan_0'=2,'chan_1'=2] {'chan_1'}, use_global_device_ids=true, to_apply=%region_7.8 | all-reduce | flops 1536 | bytes 12288 | tf_op jit(solution)/shard_map/psum | solution.py:35
  55.9 5.3 %all-reduce.13 = (f32[512]{0:T(512)S(1)}, f32[512]{0:T(512)S(1)}, f32[512]{0:T(512)S(1)}) all-reduce(f32[512]{0:T(512)S(1)} %squeeze.95, f32[512]{0:T(512)S(1)} %squeeze.96, f32[512]{0:T(512)S(1)} %squeeze.97), channel_id=1, replica_groups=mesh['blk_0'=2,'blk_1'=4,'blk_2'=8,'chan_0'=2,'chan_1'=2] {'blk_0'}, use_global_device_ids=true, to_apply=%region_18.19 | all-reduce | flops 1536 | bytes 12288 | tf_op jit(solution)/shard_map/psum | solution.py:35
  61.3 6.1 %all-reduce.4 = (f32[512]{0:T(512)S(1)}, f32[512]{0:T(512)S(1)}, f32[512]{0:T(512)S(1)}) all-reduce(f32[512]{0:T(512)S(1)} %get-tuple-element.178, f32[512]{0:T(512)S(1)} %get-tuple-element.179, f32[512]{0:T(512)S(1)} %get-tuple-element.180), channel_id=1, replica_groups=mesh['blk_0'=2,'blk_1'=4,'blk_2'=8,'chan_0'=2,'chan_1'=2] {'blk_1'}, use_global_device_ids=true, to_apply=%region_19.20 | all-reduce | flops 1536 | bytes 12288 | tf_op jit(solution)/shard_map/psum | solution.py:35
  67.3 10.9 %all-reduce.1 = (f32[512]{0:T(512)S(1)}, f32[512]{0:T(512)S(1)}, f32[512]{0:T(512)S(1)}) all-reduce(f32[512]{0:T(512)S(1)} %get-tuple-element.151, f32[512]{0:T(512)S(1)} %get-tuple-element.152, f32[512]{0:T(512)S(1)} %get-tuple-element.153), channel_id=1, replica_groups=mesh['blk_0'=2,'blk_1'=4,'blk_2'=8,'chan_0'=2,'chan_1'=2] {'blk_2'}, use_global_device_ids=true, to_apply=%region_20.21 | all-reduce | flops 1536 | bytes 12288 | tf_op jit(solution)/shard_map/psum | solution.py:35
  78.2 4.1 all-reduce.10
  82.4 9.7 %all-reduce.7 = (f32[512]{0:T(512)S(1)}, f32[512]{0:T(512)S(1)}, f32[512]{0:T(512)S(1)}) all-reduce(f32[512]{0:T(512)S(1)} %get-tuple-element.169, f32[512]{0:T(512)S(1)} %get-tuple-element.170, f32[512]{0:T(512)S(1)} %get-tuple-element.171), channel_id=1, replica_groups=mesh['blk_0'=2,'blk_1'=4,'blk_2'=8,'chan_0'=2,'chan_1'=2] {'chan_1'}, use_global_device_ids=true, to_apply=%region_22.23 | all-reduce | flops 1536 | bytes 12288 | tf_op jit(solution)/shard_map/psum | solution.py:35
  95.1 5.3 %all-reduce.12 = (f32[512]{0:T(512)S(1)}, f32[512]{0:T(512)S(1)}, f32[512]{0:T(512)S(1)}) all-reduce(f32[512]{0:T(512)S(1)} %squeeze.102, f32[512]{0:T(512)S(1)} %squeeze.103, f32[512]{0:T(512)S(1)} %squeeze.104), channel_id=1, replica_groups=mesh['blk_0'=2,'blk_1'=4,'blk_2'=8,'chan_0'=2,'chan_1'=2] {'blk_0'}, use_global_device_ids=true, to_apply=%region_33.34 | all-reduce | flops 1536 | bytes 12288 | tf_op jit(solution)/shard_map/psum | solution.py:35
  100.4 7.9 %all-reduce.3 = (f32[512]{0:T(512)S(1)}, f32[512]{0:T(512)S(1)}, f32[512]{0:T(512)S(1)}) all-reduce(f32[512]{0:T(512)S(1)} %get-tuple-element.175, f32[512]{0:T(512)S(1)} %get-tuple-element.176, f32[512]{0:T(512)S(1)} %get-tuple-element.177), channel_id=1, replica_groups=mesh['blk_0'=2,'blk_1'=4,'blk_2'=8,'chan_0'=2,'chan_1'=2] {'blk_1'}, use_global_device_ids=true, to_apply=%region_34.35 | all-reduce | flops 1536 | bytes 12288 | tf_op jit(solution)/shard_map/psum | solution.py:35
  108.3 12.5 %all-reduce = (f32[512]{0:T(512)S(1)}, f32[512]{0:T(512)S(1)}, f32[512]{0:T(512)S(1)}) all-reduce(f32[512]{0:T(512)S(1)} %get-tuple-element.148, f32[512]{0:T(512)S(1)} %get-tuple-element.149, f32[512]{0:T(512)S(1)} %get-tuple-element.150), channel_id=1, replica_groups=mesh['blk_0'=2,'blk_1'=4,'blk_2'=8,'chan_0'=2,'chan_1'=2] {'blk_2'}, use_global_device_ids=true, to_apply=%region_35.36 | all-reduce | flops 1536 | bytes 12288 | tf_op jit(solution)/shard_map/psum | solution.py:35
  120.9 3.8 all-reduce.9
  124.7 10.5 %all-reduce.6 = (f32[512]{0:T(512)S(1)}, f32[512]{0:T(512)S(1)}, f32[512]{0:T(512)S(1)}) all-reduce(f32[512]{0:T(512)S(1)} %get-tuple-element.166, f32[512]{0:T(512)S(1)} %get-tuple-element.167, f32[512]{0:T(512)S(1)} %get-tuple-element.168), channel_id=1, replica_groups=mesh['blk_0'=2,'blk_1'=4,'blk_2'=8,'chan_0'=2,'chan_1'=2] {'chan_1'}, use_global_device_ids=true, to_apply=%region_37.38 | all-reduce | flops 1536 | bytes 12288 | tf_op jit(solution)/shard_map/psum | solution.py:35
  135.8 0.9 copy-done.1
  138.0 0.8 copy-done.2
  139.0 100.9 %gather_fusion.1 = bf16[16384]{0:T(1024)(128)(2,1)S(1)} fusion(bf16[32768]{0:T(1024)(128)(2,1)S(1)} %multiply_convert_fusion, s32[16384]{0:T(1024)S(1)} %broadcast_clamp_fusion), kind=kCustom, calls=%fused_computation.1 | custom fusion | bytes 131072 | tf_op jit(solution)/shard_map/gather | solution.py:183
  240.0 100.9 %gather_fusion = bf16[16384]{0:T(1024)(128)(2,1)S(1)} fusion(bf16[32768]{0:T(1024)(128)(2,1)S(1)} %get-tuple-element.186, s32[16384]{0:T(1024)S(1)} %broadcast_clamp_fusion), kind=kCustom, calls=%fused_computation | custom fusion | bytes 131072 | tf_op jit(solution)/shard_map/gather | solution.py:182
  341.5 0.7 reduce.12
  342.1 0.6 reshape.441
  342.8 7.2 %all-to-all-start.1 = ((bf16[64,2,256]{2,1,0:T(2,128)(2,1)}), bf16[64,2,256]{2,1,0:T(2,128)(2,1)S(1)}, u32[]{:S(2)}, u32[]{:S(2)}) async-start(bf16[64,2,256]{2,1,0:T(2,128)(2,1)} %reshape.441), calls=%async_computation.1 | async-start | bytes 131072 | tf_op jit(solution)/shard_map/all_to_all | solution.py:24
  350.1 0.7 all_to_all.16
  350.8 10.3 %all-to-all-done.1 = bf16[64,2,256]{2,1,0:T(2,128)(2,1)S(1)} async-done(((bf16[64,2,256]{2,1,0:T(2,128)(2,1)}), bf16[64,2,256]{2,1,0:T(2,128)(2,1)S(1)}, u32[]{:S(2)}, u32[]{:S(2)}) %all-to-all-start.1) | async-done | bytes 65568 | tf_op jit(solution)/shard_map/all_to_all | solution.py:24
  361.1 4.8 %all-to-all-start = ((s32[64,1,512]{2,1,0:T(1,128)}), s32[64,1,512]{2,1,0:T(1,128)S(1)}, u32[]{:S(2)}, u32[]{:S(2)}) async-start(s32[64,1,512]{2,1,0:T(1,128)} %all_to_all.16), calls=%async_computation | async-start | bytes 262144 | tf_op jit(solution)/shard_map/all_to_all | solution.py:24
  365.9 0.6 pad_maximum_fusion
  366.6 10.6 %all-to-all-done = s32[64,1,512]{2,1,0:T(1,128)S(1)} async-done(((s32[64,1,512]{2,1,0:T(1,128)}), s32[64,1,512]{2,1,0:T(1,128)S(1)}, u32[]{:S(2)}, u32[]{:S(2)}) %all-to-all-start) | async-done | bytes 131104 | tf_op jit(solution)/shard_map/all_to_all | solution.py:24
  377.3 63.7 %while.14 = (s32[]{:T(128)}, f32[2,128,128]{1,2,0:T(8,128)S(1)}, s32[8,8,256]{2,1,0:T(8,128)S(1)}, bf16[8,8,256]{2,1,0:T(8,128)(2,1)S(1)}, bf16[8,8,256]{2,1,0:T...) while((s32[]{:T(128)}, f32[2,128,128]{1,2,0:T(8,128)S(1)}, ...), condition=%wide.region_49.50_spmd.clone, body=%wide.region_48.49_spmd.clone.sunk | while | flops 139800576 | bytes 2449511 | solution.py:72
  377.3 3.8 fusion.218
  381.2 4.1 fusion.219
  385.3 3.8 fusion.218
  389.1 4.1 fusion.219
  393.3 3.8 fusion.218
  397.1 4.1 fusion.219
  401.2 3.8 fusion.218
  405.0 4.1 fusion.219
  409.2 3.8 fusion.218
  413.0 4.1 fusion.219
  417.1 3.8 fusion.218
  421.0 4.1 fusion.219
  425.1 3.8 fusion.218
  428.9 4.1 fusion.219
  433.0 3.8 fusion.218
  436.9 4.1 fusion.219
  441.0 0.8 copy.14
  (168 shorter events, 12.4 us)
Async XLA Ops:
  0.6 0.7 copy-start.4
  2.8 0.7 copy-start.5
  2.8 0.7 copy-start.6
  95.0 40.8 %copy-start = (bf16[2,2,16,1024]{3,2,1,0:T(8,128)(2,1)S(1)}, bf16[2,2,16,1024]{3,2,1,0:T(8,128)(2,1)}, u32[]{:S(2)}) copy-start(bf16[2,2,16,1024]{3,2,1,0:T(8,128)(2,1)} %param.11) | copy-start | bytes 393220
  135.8 0.9 copy-start.1
  138.0 0.8 copy-start.2
  342.1 7.9 %copy-start.3 = (s32[2,1,1,64,256]{4,3,2,1,0:T(8,128)S(1)}, s32[2,1,1,64,256]{4,3,2,1,0:T(8,128)}, u32[]{:S(2)}) copy-start(s32[2,1,1,64,256]{4,3,2,1,0:T(8,128)} %param.17) | copy-start | bytes 393220
  342.8 18.3 %all-to-all-start.1 = ((bf16[64,2,256]{2,1,0:T(2,128)(2,1)}), bf16[64,2,256]{2,1,0:T(2,128)(2,1)S(1)}, u32[]{:S(2)}, u32[]{:S(2)}) async-start(bf16[64,2,256]{2,1,0:T(2,128)(2,1)} %reshape.441), calls=%async_computation.1 | async-start | bytes 131072 | tf_op jit(solution)/shard_map/all_to_all | solution.py:24
  361.1 16.1 %all-to-all-start = ((s32[64,1,512]{2,1,0:T(1,128)}), s32[64,1,512]{2,1,0:T(1,128)S(1)}, u32[]{:S(2)}, u32[]{:S(2)}) async-start(s32[64,1,512]{2,1,0:T(1,128)} %all_to_all.16), calls=%async_computation | async-start | bytes 262144 | tf_op jit(solution)/shard_map/all_to_all | solution.py:24
where the time goes:
time: 443 us; the launch traced here: 442 us
  local copies, waits for them, and re-layouts  210 us (47%)
  blocking collectives  122 us (28%)
  matrix products  40.6 us (9%)
  other arithmetic  33.9 us (8%)
  waiting for transfers between devices  20.9 us (5%)
  starting transfers between devices  12 us (3%)
    psum x15, blocking collectives, over_axes(): return functools.reduce(lax.psum, axes, shard)  122 us
    gather x2, local copies, waits for them, and re-layouts, shards(): rows_imag = jnp.where(live_rows, resid_imag[safe_rows], 0.0)  101 us
    gather x2, local copies, waits for them, and re-layouts, shards(): rows_real = jnp.where(live_rows, resid_real[safe_rows], 0.0)  101 us
    dot_general x8, matrix products, grid_piece(): jnp.einsum('grx,grcy->gcxy', kernel_u, weighted, preferred_element_type=j...  32.5 us
    another operation x8, other arithmetic  30.6 us
    all_to_all x2, waiting for transfers between devices, sent_together(): lax.all_to_all(both, axis, split_axis=split_dim, concat_axis=concat_dim,...  20.9 us
    all_to_all x2, starting transfers between devices, sent_together(): lax.all_to_all(both, axis, split_axis=split_dim, concat_axis=concat_dim,...  12 us
  transfers between devices with their start and end apart: 2, of which 2 were waited for; matrix products, arithmetic and copies ran while one was open for 0% of the time, Pallas kernels for 0%

commit v1 on v0

v1 whole, which is shorter than its diff:
```python
import math

import jax
import jax.numpy as jnp
from jax import lax
from jax.experimental import pallas as pl
from jax.experimental.pallas import tpu as pltpu
from jax.sharding import Mesh
from jax.sharding import PartitionSpec as P

S = 512
BS = 32
NB = 16
ITERS = 3
TS = 128
NT = 64
CH = 16
F32 = jnp.float32
BF16 = jnp.bfloat16
I32 = jnp.int32
MESH = pl.DeviceIdType.MESH
BLK = ("blk_0", "blk_1", "blk_2")
CHAN = ("chan_0", "chan_1")
VM = pl.BlockSpec(memory_space=pltpu.VMEM)
SM = pl.BlockSpec(memory_space=pltpu.SMEM)


def iota(shape, axis):
    return lax.broadcasted_iota(I32, shape, axis)


def sums_and_tables(pm_ref, vis_ref, mod_ref, flag_ref, pq_ref, table_ref):
    for slot in range(2):
        first = pm_ref[slot, 0]
        second = pm_ref[slot, 1]
        same = (first == second).astype(F32)
        lane = iota((1, 128), 1)
        planes = [[], [], [], []]
        for tb in range(8):
            at = slice(tb * 128, tb * 128 + 128)
            base = lane + tb * 128
            diagonal = ((base >> 5) == (base & 31)).astype(F32)
            weight = flag_ref[slot, :, at].astype(F32) * (1.0 - same * diagonal)
            vr = vis_ref[0, slot, :, at].astype(F32) * weight
            vi = vis_ref[1, slot, :, at].astype(F32) * weight
            mr = mod_ref[0, slot, :, at].astype(F32) * weight
            mi = mod_ref[1, slot, :, at].astype(F32) * weight
            sums = (
                jnp.sum(vr * mr + vi * mi, axis=0, keepdims=True),
                jnp.sum(vi * mr - vr * mi, axis=0, keepdims=True),
                jnp.sum(mr * mr + mi * mi, axis=0, keepdims=True),
            )
            col = slice((tb % 2) * 128, (tb % 2) * 128 + 128)
            for q in range(3):
                row = slot * 3 + q
                pq_ref[tb // 2, row : row + 1, col] = sums[q]
            for plane, value in zip(planes, (vr, vi, mr, mi)):
                plane.append(value)
        for q in range(4):
            table = jnp.concatenate(planes[q], axis=0)
            table_ref[q * 128 : q * 128 + 128, slot * 128 : slot * 128 + 128] = table.T.astype(BF16)
        for quarter in range(4):
            col = slice(slot * 128, slot * 128 + 128)
            pq_ref[quarter, 6:7, col] = jnp.full((1, 128), first.astype(F32))
            pq_ref[quarter, 7:8, col] = jnp.full((1, 128), second.astype(F32))


def gather_tile(tile, index_ref, codes_ref, table_ref, rows_ref, ints_ref):
    index = index_ref[pl.ds(tile, 1), :]
    hi = ((index >> 14) << 7) | (((index >> 7) & 7) << 4) | ((index >> 10) & 15)
    onehot = jnp.where(iota((256, 256), 0) == hi, 1.0, 0.0).astype(BF16)
    lifted = jnp.dot(table_ref[...], onehot, preferred_element_type=F32)
    low_high = (index >> 3) & 15
    low_low = index & 7
    live = iota((8, 256), 0) == low_low
    pieces = []
    masks = [jnp.broadcast_to(low_high == k, (8, 256)) for k in range(16)]
    for q in range(4):
        part = lifted[q * 128 : q * 128 + 8]
        for k in range(1, 16):
            part = jnp.where(masks[k], lifted[q * 128 + k * 8 : q * 128 + k * 8 + 8], part)
        value = jnp.sum(jnp.where(live, part, 0.0), axis=0, keepdims=True)
        pieces += [value[:, :128], value[:, 128:]]
    rows_ref[tile] = jnp.concatenate(pieces, axis=0).astype(BF16)
    u = codes_ref[0, pl.ds(tile, 1), :]
    v = codes_ref[1, pl.ds(tile, 1), :]
    both = u | (v << 16)
    place = (((index >> 14) & 1) << 10) | (index & 1023)
    ints_ref[tile] = jnp.concatenate([both[:, :128], both[:, 128:], place[:, :128], place[:, 128:]], axis=0)


def sender_kernel(pm_ref, vis_ref, mod_ref, flag_ref, index_ref, codes_ref, pq_ref, rows_ref, ints_ref, table_ref):
    sums_and_tables(pm_ref, vis_ref, mod_ref, flag_ref, pq_ref, table_ref)

    def step(tile, carry):
        gather_tile(tile, index_ref, codes_ref, table_ref, rows_ref, ints_ref)
        return carry

    lax.fori_loop(0, NT, step, 0)


def sender(pm, vis, mod, flag, index, codes):
    return pl.pallas_call(
        sender_kernel,
        name="sender",
        out_shape=(
            jax.ShapeDtypeStruct((4, 8, 256), F32),
            jax.ShapeDtypeStruct((NT, 8, 128), BF16),
            jax.ShapeDtypeStruct((NT, 4, 128), I32),
        ),
        in_specs=[SM, VM, VM, VM, VM, VM],
        out_specs=(VM, VM, VM),
        scratch_shapes=[pltpu.VMEM((512, 256), BF16)],
    )(pm, vis, mod, flag, index, codes)


def exchange_kernel(
    pq_ref, rows_ref, ints_ref, all_ref, got_rows, got_ints, part, send_sem, recv_sem, a2a_send, a2a_recv, own_sem
):
    xh, y, z = lax.axis_index("blk_0"), lax.axis_index("blk_1"), lax.axis_index("blk_2")
    xl, core = lax.axis_index("chan_0"), lax.axis_index("chan_1")
    me = (xh * 4 + y) * 8 + z
    x = xh * 2 + xl
    quarter = xl * 2 + core

    def tile_id(step):
        t = lax.rem(me + step, NT)
        return t, {"blk_0": t // 32, "blk_1": lax.rem(t // 8, 4), "blk_2": lax.rem(t, 8)}

    def chan_id(step):
        c = lax.rem(quarter + step, 4)
        return c, {"chan_0": c // 2, "chan_1": lax.rem(c, 2)}

    def x_id(step):
        other = lax.rem(x + step, 4)
        return other, {"blk_0": other // 2, "chan_0": lax.rem(other, 2)}

    barrier = pltpu.get_barrier_semaphore()

    def greet(step, carry):
        pl.semaphore_signal(barrier, inc=1, device_id=tile_id(step)[1], device_id_type=MESH)
        return carry

    lax.fori_loop(1, NT, greet, 0)
    for step in range(1, 4):
        pl.semaphore_signal(barrier, inc=1, device_id=chan_id(step)[1], device_id_type=MESH)
        pl.semaphore_signal(barrier, inc=1, device_id=x_id(step)[1], device_id_type=MESH)
    pl.semaphore_wait(barrier, NT - 1 + 6)

    def remote(src, dst, k, device):
        return pltpu.make_async_remote_copy(
            src_ref=src,
            dst_ref=dst,
            send_sem=send_sem.at[k],
            recv_sem=recv_sem.at[k],
            device_id=device,
            device_id_type=MESH,
        )

    for step in range(1, 4):
        c, device = chan_id(step)
        remote(pq_ref.at[c], part.at[step - 1], step - 1, device).start()

    def send_tile(step, carry):
        t, device = tile_id(step)
        pltpu.make_async_remote_copy(
            src_ref=rows_ref.at[t], dst_ref=got_rows.at[me], send_sem=a2a_send.at[0],
            recv_sem=a2a_recv.at[0], device_id=device, device_id_type=MESH,
        ).start()
        pltpu.make_async_remote_copy(
            src_ref=ints_ref.at[t], dst_ref=got_ints.at[me], send_sem=a2a_send.at[1],
            recv_sem=a2a_recv.at[1], device_id=device, device_id_type=MESH,
        ).start()
        return carry

    total = pq_ref[quarter]
    for step in range(1, 4):
        c, device = chan_id(step)
        remote(pq_ref.at[c], part.at[step - 1], step - 1, device).wait()
        total = total + part[step - 1]
    total = jnp.concatenate([total[:6], pq_ref[0, 6:8, :]], axis=0)
    mine = jnp.concatenate([total[:, :128], total[:, 128:]], axis=0).astype(BF16)
    all_ref[core, x, y, z] = mine

    for step in range(1, 8):
        remote(all_ref.at[core, x, y, z], all_ref.at[core, x, y, z], 3, {"blk_2": lax.rem(z + step, 8)}).start()
    lax.fori_loop(1, NT, send_tile, 0)
    keep_rows = pltpu.make_async_copy(rows_ref.at[me], got_rows.at[me], own_sem.at[0])
    keep_ints = pltpu.make_async_copy(ints_ref.at[me], got_ints.at[me], own_sem.at[1])
    keep_rows.start()
    keep_ints.start()
    line = all_ref.at[core, x, y, pl.ds(0, 7)]
    remote(line, line, 3, {"blk_2": lax.rem(z + 1, 8)}).wait()

    plane = all_ref.at[core, x, y]
    for step in range(1, 4):
        remote(plane, plane, 4, {"blk_1": lax.rem(y + step, 4)}).start()
    span = all_ref.at[core, x, pl.ds(0, 3)]
    remote(span, span, 4, {"blk_1": lax.rem(y + 1, 4)}).wait()

    slab = all_ref.at[core, x]
    for step in range(1, 4):
        remote(slab, slab, 5, x_id(step)[1]).start()
    span = all_ref.at[core, pl.ds(0, 3)]
    remote(span, span, 5, x_id(1)[1]).wait()

    half = all_ref.at[core]
    other = {"chan_1": 1 - core}
    copy = remote(half, half, 6, other)
    copy.start()
    copy.wait()

    keep_rows.wait()
    keep_ints.wait()
    for buf, k in ((got_rows, 0), (got_ints, 1)):
        span = buf.at[pl.ds(0, NT - 1)]
        pltpu.make_async_remote_copy(
            src_ref=span, dst_ref=span, send_sem=a2a_send.at[k],
            recv_sem=a2a_recv.at[k], device_id=other, device_id_type=MESH,
        ).wait()


def exchange(pq, rows, ints):
    return pl.pallas_call(
        exchange_kernel,
        name="exchange",
        out_shape=(
            jax.ShapeDtypeStruct((2, 4, 4, 8, 16, 128), BF16),
            jax.ShapeDtypeStruct((NT, 8, 128), BF16),
            jax.ShapeDtypeStruct((NT, 4, 128), I32),
        ),
        in_specs=[VM, VM, VM],
        out_specs=(VM, VM, VM),
        scratch_shapes=[
            pltpu.VMEM((3, 8, 256), F32),
            pltpu.SemaphoreType.DMA((7,)),
            pltpu.SemaphoreType.DMA((7,)),
            pltpu.SemaphoreType.DMA((2,)),
            pltpu.SemaphoreType.DMA((2,)),
            pltpu.SemaphoreType.DMA((2,)),
        ],
        compiler_params=pltpu.CompilerParams(collective_id=0, has_side_effects=True),
    )(pq, rows, ints)


def solve(wide_ref, gain_ref, p_refs):
    def lines(core, xl, half, slot, part):
        out = []
        for xh in range(2):
            group = core * 4 + xh * 2 + xl
            out.append(wide_ref[pl.ds(group * 512 + half * 8 + slot * 3 + part, 32, stride=16), :])
        return out

    for core in range(2):
        for xl in range(2):
            for half in range(2):
                tb = (xl * 2 + core) * 2 + half
                for part in range(3):
                    block = lines(core, xl, half, 0, part) + lines(core, xl, half, 1, part)
                    p_refs[part][tb * 128 : tb * 128 + 128, :] = jnp.concatenate(block, axis=0).T

    def pair_lines(side):
        out = []
        for slot in range(2):
            for xh in range(2):
                out.append(wide_ref[pl.ds((xh * 2) * 512 + slot * 8 + 6 + side, 32, stride=16), :])
        return out

    lane = iota((128, 128), 1).astype(F32)
    blocks = [pair_lines(0), pair_lines(1)]
    columns = [jnp.concatenate(b, axis=0) for b in blocks]
    onehot = jnp.concatenate([(c == lane).astype(F32) for c in columns], axis=0)
    rows = [c.T[:32].astype(I32) for c in columns]

    def spread(g, which):
        return jnp.take_along_axis(g, rows[which], axis=1)

    pr_ref, pi_ref, q_ref = p_refs
    gr = gain_ref[0]
    gi = gain_ref[1]
    for sweep in range(ITERS):
        ar, ai, br, bi = spread(gr, 0), spread(gi, 0), spread(gr, 1), spread(gi, 1)
        a2 = ar * ar + ai * ai
        b2 = br * br + bi * bi
        zero = jnp.zeros((32, 128), F32)
        first = [zero, zero, zero]
        second = [zero, zero, zero]
        for i in range(32):
            pr = pr_ref[i * 32 : i * 32 + 32, :]
            pi = pi_ref[i * 32 : i * 32 + 32, :]
            q = q_ref[i * 32 : i * 32 + 32, :]
            xr, xi, x2 = ar[i : i + 1], ai[i : i + 1], a2[i : i + 1]
            second[0] = second[0] + (pr * xr + pi * xi)
            second[1] = second[1] + (pr * xi - pi * xr)
            second[2] = second[2] + q * x2
        for j in range(32):
            at = pl.ds(j, 32, stride=32)
            pr, pi, q = pr_ref[at, :], pi_ref[at, :], q_ref[at, :]
            xr, xi, x2 = br[j : j + 1], bi[j : j + 1], b2[j : j + 1]
            first[0] = first[0] + (pr * xr - pi * xi)
            first[1] = first[1] + (pr * xi + pi * xr)
            first[2] = first[2] + q * x2
        terms = jnp.concatenate([jnp.concatenate(first, axis=0), jnp.concatenate(second, axis=0)], axis=1)
        total = jnp.dot(terms, onehot, precision=lax.Precision.HIGHEST, preferred_element_type=F32)
        denominator = jnp.where(iota((32, 128), 1) < NB, total[64:96], 1.0)
        ur = total[0:32] / denominator
        ui = total[32:64] / denominator
        if sweep % 2 == 1:
            gr, gi = 0.5 * (ur + gr), 0.5 * (ui + gi)
        else:
            gr, gi = ur, ui
    return gr, gi


def residual_rows(gr, gi, wide_ref, lines_ref, ints_ref, res_ref):
    turned_r = gr.T[:NB, :]
    turned_i = gi.T[:NB, :]
    turned_r = jnp.concatenate([turned_r] * 4, axis=1)
    turned_i = jnp.concatenate([turned_i] * 4, axis=1)

    def blocks(slot, side):
        return jnp.concatenate(
            [wide_ref[pl.ds((xh * 2) * 512 + slot * 8 + 6 + side, 32, stride=16), :] for xh in range(2)], axis=0
        )

    lane = iota((NT, 128), 1)
    which = jnp.where(
        lane < 64,
        jnp.where(lane < 32, blocks(0, 0), blocks(1, 0)),
        jnp.where(lane < 96, blocks(0, 1), blocks(1, 1)),
    ).astype(I32)
    table_r = jnp.zeros((NT, 128), F32)
    table_i = jnp.zeros((NT, 128), F32)
    for n in range(NB):
        hit = which == n
        table_r = jnp.where(hit, turned_r[n : n + 1], table_r)
        table_i = jnp.where(hit, turned_i[n : n + 1], table_i)
    for half in range(2):
        place = ints_ref[pl.ds(2 + half, NT, stride=4), :]
        slot = (place >> 10) * 32
        at_a = slot + ((place >> 5) & 31)
        at_b = slot + (place & 31) + 64
        ar = jnp.take_along_axis(table_r, at_a, axis=1)
        ai = jnp.take_along_axis(table_i, at_a, axis=1)
        br = jnp.take_along_axis(table_r, at_b, axis=1)
        bi = jnp.take_along_axis(table_i, at_b, axis=1)
        vr, vi, mr, mi = (lines_ref[pl.ds(q * 2 + half, NT, stride=8), :] for q in range(4))
        twisted_r = mr * br + mi * bi
        twisted_i = mi * br - mr * bi
        res_ref[0, half] = (vr - (ar * twisted_r - ai * twisted_i)).astype(BF16).astype(F32)
        res_ref[1, half] = (vi - (ar * twisted_i + ai * twisted_r)).astype(BF16).astype(F32)


def window(code):
    shifted = iota((8, 128), 0) * 8 - code
    block = (32 - shifted) >> 6
    distance = block * 64 + shifted
    angle = distance.astype(F32) * (math.pi / 64)
    z = angle * angle
    cos = 1.0 / math.factorial(14)
    for k in range(6, -1, -1):
        cos = 1.0 / math.factorial(2 * k) - z * cos
    value = jnp.where(jnp.abs(distance) < 32, cos * cos, 0.0).astype(BF16).astype(F32)
    return block, value


def owner_kernel(all_ref, rows_ref, ints_ref, gain_ref, grid_ref, solved_ref, wide_ref, pr_ref, pi_ref, q_ref, lines_ref, res_ref):
    wide_ref[...] = all_ref[...].astype(F32)
    lines_ref[...] = rows_ref[...].astype(F32)
    gr, gi = solve(wide_ref, gain_ref, (pr_ref, pi_ref, q_ref))
    solved_ref[0] = gr.T[:NB, :]
    solved_ref[1] = gi.T[:NB, :]
    residual_rows(gr, gi, wide_ref, lines_ref, ints_ref, res_ref)

    def step(group, acc):
        lefts, rights = [], []
        for member in range(4):
            s = group * 4 + member
            for half in range(2):
                both = ints_ref[pl.ds(s * 4 + half, 1), :]
                ublock, uvalue = window(both & 65535)
                vblock, vvalue = window(both >> 16)
                hr = (vvalue * res_ref[0, half, pl.ds(s, 1), :]).astype(BF16).astype(F32)
                hi = (vvalue * res_ref[1, half, pl.ds(s, 1), :]).astype(BF16).astype(F32)
                lefts.append(
                    jnp.concatenate([jnp.where(ublock == k, uvalue, 0.0) for k in range(16)], axis=0).astype(BF16)
                )
                hits = [vblock == k for k in range(16)]
                rights.append(
                    jnp.concatenate(
                        [jnp.where(hit, hr, 0.0) for hit in hits] + [jnp.where(hit, hi, 0.0) for hit in hits], axis=0
                    ).astype(BF16)
                )
        left = jnp.concatenate(lefts, axis=1)
        right = jnp.concatenate(rights, axis=1)
        return acc + lax.dot_general(left, right, (((1,), (1,)), ((), ())), preferred_element_type=F32)

    acc = lax.fori_loop(0, NT // 4, step, jnp.zeros((TS, 2 * TS), F32))
    grid_ref[0] = acc[:, :TS]
    grid_ref[1] = acc[:, TS:]


def owner(everything, rows, ints, gains):
    return pl.pallas_call(
        owner_kernel,
        name="owner",
        out_shape=(
            jax.ShapeDtypeStruct((2, TS, TS), F32),
            jax.ShapeDtypeStruct((2, NB, BS), F32),
        ),
        in_specs=[VM, VM, VM, VM],
        out_specs=(VM, VM),
        scratch_shapes=[
            pltpu.VMEM((4096, 128), F32),
            pltpu.VMEM((1024, 128), F32),
            pltpu.VMEM((1024, 128), F32),
            pltpu.VMEM((1024, 128), F32),
            pltpu.VMEM((512, 128), F32),
            pltpu.VMEM((2, 2, NT, 128), F32),
        ],
    )(everything.reshape(4096, 128), rows.reshape(512, 128), ints.reshape(256, 128), gains)


def start_gains(gain_amp, gain_phase):
    both = jnp.stack((gain_amp * jnp.cos(gain_phase), gain_amp * jnp.sin(gain_phase)))
    turned = both.reshape(2, NB, BS).transpose(0, 2, 1)
    return jnp.pad(turned, ((0, 0), (0, 0), (0, 128 - NB)))


def shards(pair_map, visibilities, model_vis, flag_mask, gain_amp, gain_phase, row_index, cell_codes):
    gains = start_gains(gain_amp, gain_phase)
    pq, rows, ints = sender(
        pair_map, visibilities, model_vis, flag_mask, row_index[0, 0], cell_codes.reshape(2, NT, 256)
    )
    everything, got_rows, got_ints = exchange(pq, rows, ints)
    grid, solved = owner(everything, got_rows, got_ints, gains)
    return grid[None, None], solved.reshape(2, S)


def solution(mesh):
    split = Mesh(mesh.devices.reshape(2, 4, 8, 2, 2), BLK + CHAN)
    placed = (
        P(BLK, None),
        P(None, BLK, CHAN, None),
        P(None, BLK, CHAN, None),
        P(BLK, CHAN, None),
        P(),
        P(),
        P(CHAN, BLK, None, None),
        P(None, CHAN, BLK, None, None),
    )
    return jax.shard_map(
        shards,
        mesh=split,
        in_specs=placed,
        out_specs=(P(CHAN, BLK, None, None, None), P()),
        check_vma=False,
    )
```

time: 443 us -> 71.1 us (0.16)
  local copies, waits for them, and re-layouts: 210 us -> 3 us
  blocking collectives: 122 us -> 0 us
  Pallas kernels: 0 us -> 67.1 us
  matrix products: 40.6 us -> 0 us
  other arithmetic: 33.9 us -> 0.05 us
  waiting for transfers between devices: 20.9 us -> 0 us
  starting transfers between devices: 12 us -> 0 us
    gather x4 -> x0, local copies, waits for them, and re-layouts: 202 us -> none  [the longest x2 101 us: shards(): rows_imag = jnp.where(live_rows, resid_imag[safe_rows], 0.0)]
    psum x15 -> x0, blocking collectives: 122 us -> none  [over_axes(): return functools.reduce(lax.psum, axes, shard)]
    pallas_call x0 -> x3, Pallas kernels: none -> 67.1 us  [the longest x1 36.9 us: exchange(): pl.pallas_call(exchange_kernel, name='exchange', out_shape=(jax.ShapeDtyp...]
    dot_general x52 -> x0, matrix products: 40.6 us -> none  [the longest x8 32.5 us: grid_piece(): jnp.einsum('grx,grcy->gcxy', kernel_u, weighted, preferred_element_type=j...]
    another operation x21 -> x0, other arithmetic: 31.2 us -> none
    all_to_all x2 -> x0, waiting for transfers between devices: 20.9 us -> none  [sent_together(): lax.all_to_all(both, axis, split_axis=split_dim, concat_axis=concat_dim,...]
    all_to_all x2 -> x0, starting transfers between devices: 12 us -> none  [sent_together(): lax.all_to_all(both, axis, split_axis=split_dim, concat_axis=concat_dim,...]
  transfers between devices with their start and end apart: 2 -> 0, of which waited for: 2 -> 0; matrix products, arithmetic and copies ran while one was open for 0% -> 0% of each run, Pallas kernels for 0% -> 0%
where the time goes in v1:
time: 71.1 us; the launch traced here: 70.8 us
  Pallas kernels  67.1 us (94%)
  local copies, waits for them, and re-layouts  3 us (4%)
    pallas_call x1, Pallas kernels, exchange(): pl.pallas_call(exchange_kernel, name='exchange', out_shape=(jax.ShapeDtyp...  36.9 us
    pallas_call x1, Pallas kernels, sender(): pl.pallas_call(sender_kernel, name='sender', out_shape=(jax.ShapeDtypeStr...  18.2 us
    pallas_call x1, Pallas kernels, owner(): pl.pallas_call(owner_kernel, name='owner', out_shape=(jax.ShapeDtypeStruc...  12 us

profile of v1, /device:TPU:1, one launch (start us, length us, event | category | flops | bytes accessed | tf_op | source)
XLA Modules:
  0.0 70.8 jit_solution(8660913696923622480)
XLA Ops:
  0.6 18.2 %sender.1 = (f32[4,8,256]{2,1,0:T(8,128)}, bf16[64,8,128]{2,1,0:T(8,128)(2,1)}, s32[64,4,128]{2,1,0:T(4,128)}) custom-call(s32[2,2]{1,0:T(2,128)} %pm_ref.1, bf16[2,2,16,1024]{3,2,1,0:T(8,128)(2,1)} %vis_ref.1, bf16[2,2,16,1024]{3,2,1,0:T(8,128)(2,1)} %mod_ref.1, s32[2,16,1024]{2,1,0:T(8,128)} %flag_ref.1, s32[64,256]{1,0:T(8,128)} %bitcast.12, ...), custom_call_target="tpu_custom_call" | custom-call | tf_op jit(solution)/shard_map/sender/pallas_call | solution.py:103
  18.8 36.9 %exchange.1 = (bf16[2,4,4,8,16,128]{5,4,3,2,1,0:T(8,128)(2,1)}, bf16[64,8,128]{2,1,0:T(8,128)(2,1)}, s32[64,4,128]{2,1,0:T(4,128)}) custom-call(f32[4,8,256]{2,1,0:T(8,128)} %get-tuple-element.10.pq_ref, bf16[64,8,128]{2,1,0:T(8,128)(2,1)} %get-tuple-element.11.rows_ref, s32[64,4,128]{2,1,0:T(4,128)} %get-tuple-element.12.ints_ref), custom_call_target="tpu_custom_call" | custom-call | tf_op jit(solution)/shard_map/exchange/pallas_call | solution.py:224
  55.8 0.0 copy-start.1
  55.8 0.0 copy-start
  55.8 0.7 copy-done.1
  56.5 0.0 copy-done
  56.5 0.1 stack.9
  56.6 0.1 copy.10
  56.7 0.1 stack.10
  56.7 0.1 copy.11
  56.8 0.6 pad.4.gain_ref
  57.5 12.0 %owner.1 = (f32[2,128,128]{2,1,0:T(8,128)}, f32[2,16,32]{2,1,0:T(8,128)}) custom-call(bf16[4096,128]{1,0:T(8,128)(2,1)} %bitcast.8, bf16[512,128]{1,0:T(8,128)(2,1)} %bitcast.10, s32[256,128]{1,0:T(8,128)} %bitcast.11, f32[2,32,128]{2,1,0:T(8,128)} %pad.4.gain_ref), custom_call_target="tpu_custom_call" | custom-call | tf_op jit(solution)/shard_map/owner/pallas_call | solution.py:404
  69.5 1.4 %reshape.28 = f32[2,512]{1,0:T(2,128)} reshape(f32[2,16,32]{2,1,0:T(8,128)} %get-tuple-element.17) | data formatting | bytes 8192 | tf_op jit(solution)/shard_map/reshape | solution.py:437
  (2 shorter events, 0.0 us)
Async XLA Ops:
  55.8 0.7 copy-start.1
  55.8 0.7 copy-start

commit v2 on v1

--- a/solution.py
+++ b/solution.py
@@ -65,16 +65,23 @@
             pq_ref[quarter, 7:8, col] = jnp.full((1, 128), second.astype(F32))
 
 
-def gather_tile(tile, index_ref, codes_ref, table_ref, rows_ref, ints_ref):
+def iota_table():
+    return iota((256, 256), 0).astype(F32).astype(BF16)
+
+
+def gather_tile(tile, index_ref, codes_ref, table_ref, iota_ref, rows_ref):
     index = index_ref[pl.ds(tile, 1), :]
     hi = ((index >> 14) << 7) | (((index >> 7) & 7) << 4) | ((index >> 10) & 15)
-    onehot = jnp.where(iota((256, 256), 0) == hi, 1.0, 0.0).astype(BF16)
+    high = jnp.broadcast_to(hi.astype(F32), (16, 256)).astype(BF16)
+    one, zero = jnp.ones((16, 256), BF16), jnp.zeros((16, 256), BF16)
+    onehot = jnp.concatenate(
+        [jnp.where(iota_ref[k * 16 : k * 16 + 16, :] == high, one, zero) for k in range(16)], axis=0
+    )
     lifted = jnp.dot(table_ref[...], onehot, preferred_element_type=F32)
     low_high = (index >> 3) & 15
-    low_low = index & 7
-    live = iota((8, 256), 0) == low_low
+    live = iota((8, 256), 0) == (index & 7)
+    masks = [jnp.broadcast_to(low_high == k, (8, 256)) for k in range(16)]
     pieces = []
-    masks = [jnp.broadcast_to(low_high == k, (8, 256)) for k in range(16)]
     for q in range(4):
         part = lifted[q * 128 : q * 128 + 8]
         for k in range(1, 16):
@@ -82,46 +89,32 @@
         value = jnp.sum(jnp.where(live, part, 0.0), axis=0, keepdims=True)
         pieces += [value[:, :128], value[:, 128:]]
     rows_ref[tile] = jnp.concatenate(pieces, axis=0).astype(BF16)
-    u = codes_ref[0, pl.ds(tile, 1), :]
-    v = codes_ref[1, pl.ds(tile, 1), :]
-    both = u | (v << 16)
+
+
+def write_ints(tile, index_ref, codes_ref, ints_ref):
+    index = index_ref[pl.ds(tile, 1), :]
+    both = codes_ref[0, pl.ds(tile, 1), :] | (codes_ref[1, pl.ds(tile, 1), :] << 16)
     place = (((index >> 14) & 1) << 10) | (index & 1023)
     ints_ref[tile] = jnp.concatenate([both[:, :128], both[:, 128:], place[:, :128], place[:, 128:]], axis=0)
 
 
-def sender_kernel(pm_ref, vis_ref, mod_ref, flag_ref, index_ref, codes_ref, pq_ref, rows_ref, ints_ref, table_ref):
-    sums_and_tables(pm_ref, vis_ref, mod_ref, flag_ref, pq_ref, table_ref)
-
-    def step(tile, carry):
-        gather_tile(tile, index_ref, codes_ref, table_ref, rows_ref, ints_ref)
-        return carry
-
-    lax.fori_loop(0, NT, step, 0)
-
-
-def sender(pm, vis, mod, flag, index, codes):
-    return pl.pallas_call(
-        sender_kernel,
-        name="sender",
-        out_shape=(
-            jax.ShapeDtypeStruct((4, 8, 256), F32),
-            jax.ShapeDtypeStruct((NT, 8, 128), BF16),
-            jax.ShapeDtypeStruct((NT, 4, 128), I32),
-        ),
-        in_specs=[SM, VM, VM, VM, VM, VM],
-        out_specs=(VM, VM, VM),
-        scratch_shapes=[pltpu.VMEM((512, 256), BF16)],
-    )(pm, vis, mod, flag, index, codes)
-
-
-def exchange_kernel(
-    pq_ref, rows_ref, ints_ref, all_ref, got_rows, got_ints, part, send_sem, recv_sem, a2a_send, a2a_recv, own_sem
+NEAR = (1, 3, 2)
+
+
+def front_kernel(
+    pm_ref, vis_ref, mod_ref, flag_ref, index_ref, codes_ref,
+    all_ref, got_rows, got_ints,
+    table_ref, iota_ref, pq_ref, rows_ref, ints_ref, part,
+    sum_send, sum_recv, line_send, line_recv, in_send, in_recv, out_send, out_recv,
+    core_send, core_recv, a2a_send, a2a_recv, own_sem,
 ):
     xh, y, z = lax.axis_index("blk_0"), lax.axis_index("blk_1"), lax.axis_index("blk_2")
     xl, core = lax.axis_index("chan_0"), lax.axis_index("chan_1")
     me = (xh * 4 + y) * 8 + z
     x = xh * 2 + xl
     quarter = xl * 2 + core
+    inner = y * (1 - core) + x * core
+    outer = x * (1 - core) + y * core
 
     def tile_id(step):
         t = lax.rem(me + step, NT)
@@ -131,9 +124,11 @@
         c = lax.rem(quarter + step, 4)
         return c, {"chan_0": c // 2, "chan_1": lax.rem(c, 2)}
 
-    def x_id(step):
-        other = lax.rem(x + step, 4)
-        return other, {"blk_0": other // 2, "chan_0": lax.rem(other, 2)}
+    def plane_id(in_step, out_step):
+        i, o = lax.rem(inner + in_step, 4), lax.rem(outer + out_step, 4)
+        py = i * (1 - core) + o * core
+        px = o * (1 - core) + i * core
+        return {"blk_0": px // 2, "chan_0": lax.rem(px, 2), "blk_1": py}
 
     barrier = pltpu.get_barrier_semaphore()
 
@@ -141,143 +136,202 @@
         pl.semaphore_signal(barrier, inc=1, device_id=tile_id(step)[1], device_id_type=MESH)
         return carry
 
-    lax.fori_loop(1, NT, greet, 0)
     for step in range(1, 4):
         pl.semaphore_signal(barrier, inc=1, device_id=chan_id(step)[1], device_id_type=MESH)
-        pl.semaphore_signal(barrier, inc=1, device_id=x_id(step)[1], device_id_type=MESH)
-    pl.semaphore_wait(barrier, NT - 1 + 6)
-
-    def remote(src, dst, k, device):
-        return pltpu.make_async_remote_copy(
-            src_ref=src,
-            dst_ref=dst,
-            send_sem=send_sem.at[k],
-            recv_sem=recv_sem.at[k],
-            device_id=device,
+        pl.semaphore_signal(
+            barrier, inc=1, device_id={"blk_0": lax.rem(x + step, 4) // 2, "chan_0": lax.rem(x + step, 2)},
             device_id_type=MESH,
         )
+    lax.fori_loop(1, NT, greet, 0)
+
+    def remote(src, dst, send, recv, device):
+        return pltpu.make_async_remote_copy(
+            src_ref=src, dst_ref=dst, send_sem=send, recv_sem=recv, device_id=device, device_id_type=MESH
+        )
+
+    def gather(first, last):
+        def step(group, carry):
+            for member in range(4):
+                gather_tile(group * 4 + member, index_ref, codes_ref, table_ref, iota_ref, rows_ref)
+            return carry
+
+        lax.fori_loop(first // 4, last // 4, step, 0)
+
+    def to_owners(src, dst, k):
+        def step(n, carry):
+            t, device = tile_id(n)
+            remote(src.at[t], dst.at[me], a2a_send.at[k], a2a_recv.at[k], device).start()
+            return carry
+
+        lax.fori_loop(1, NT, step, 0)
+
+    sums_and_tables(pm_ref, vis_ref, mod_ref, flag_ref, pq_ref, table_ref)
+    iota_ref[...] = iota_table()
+
+    def ints_step(group, carry):
+        for member in range(4):
+            write_ints(group * 4 + member, index_ref, codes_ref, ints_ref)
+        return carry
+
+    lax.fori_loop(0, NT // 4, ints_step, 0)
+    gather(0, CUT[0])
+    pl.semaphore_wait(barrier, NT - 1 + 6)
+
+    def piece(step):
+        c, device = chan_id(step)
+        return remote(pq_ref.at[c], part.at[step - 1], sum_send.at[step - 1], sum_recv.at[step - 1], device)
 
     for step in range(1, 4):
-        c, device = chan_id(step)
-        remote(pq_ref.at[c], part.at[step - 1], step - 1, device).start()
-
-    def send_tile(step, carry):
-        t, device = tile_id(step)
-        pltpu.make_async_remote_copy(
-            src_ref=rows_ref.at[t], dst_ref=got_rows.at[me], send_sem=a2a_send.at[0],
-            recv_sem=a2a_recv.at[0], device_id=device, device_id_type=MESH,
-        ).start()
-        pltpu.make_async_remote_copy(
-            src_ref=ints_ref.at[t], dst_ref=got_ints.at[me], send_sem=a2a_send.at[1],
-            recv_sem=a2a_recv.at[1], device_id=device, device_id_type=MESH,
-        ).start()
-        return carry
-
+        piece(step).start()
+    to_owners(ints_ref, got_ints, 1)
+    keep_ints = pltpu.make_async_copy(ints_ref.at[me], got_ints.at[me], own_sem.at[1])
+    keep_ints.start()
+    gather(CUT[0], CUT[1])
     total = pq_ref[quarter]
     for step in range(1, 4):
-        c, device = chan_id(step)
-        remote(pq_ref.at[c], part.at[step - 1], step - 1, device).wait()
+        piece(step).wait_recv()
         total = total + part[step - 1]
     total = jnp.concatenate([total[:6], pq_ref[0, 6:8, :]], axis=0)
-    mine = jnp.concatenate([total[:, :128], total[:, 128:]], axis=0).astype(BF16)
-    all_ref[core, x, y, z] = mine
-
+    all_ref[core, outer, inner, z] = jnp.concatenate([total[:, :128], total[:, 128:]], axis=0).astype(BF16)
+
+    mine = all_ref.at[core, outer, inner, z]
     for step in range(1, 8):
-        remote(all_ref.at[core, x, y, z], all_ref.at[core, x, y, z], 3, {"blk_2": lax.rem(z + step, 8)}).start()
-    lax.fori_loop(1, NT, send_tile, 0)
+        remote(mine, mine, line_send.at[0], line_recv.at[0], {"blk_2": lax.rem(z + step, 8)}).start()
+    gather(CUT[1], NT)
+    to_owners(rows_ref, got_rows, 0)
     keep_rows = pltpu.make_async_copy(rows_ref.at[me], got_rows.at[me], own_sem.at[0])
-    keep_ints = pltpu.make_async_copy(ints_ref.at[me], got_ints.at[me], own_sem.at[1])
     keep_rows.start()
-    keep_ints.start()
-    line = all_ref.at[core, x, y, pl.ds(0, 7)]
-    remote(line, line, 3, {"blk_2": lax.rem(z + 1, 8)}).wait()
-
-    plane = all_ref.at[core, x, y]
-    for step in range(1, 4):
-        remote(plane, plane, 4, {"blk_1": lax.rem(y + step, 4)}).start()
-    span = all_ref.at[core, x, pl.ds(0, 3)]
-    remote(span, span, 4, {"blk_1": lax.rem(y + 1, 4)}).wait()
-
-    slab = all_ref.at[core, x]
-    for step in range(1, 4):
-        remote(slab, slab, 5, x_id(step)[1]).start()
-    span = all_ref.at[core, pl.ds(0, 3)]
-    remote(span, span, 5, x_id(1)[1]).wait()
-
-    half = all_ref.at[core]
-    other = {"chan_1": 1 - core}
-    copy = remote(half, half, 6, other)
-    copy.start()
-    copy.wait()
-
+    seven = all_ref.at[core, outer, inner, pl.ds(0, 7)]
+    line = remote(seven, seven, line_send.at[0], line_recv.at[0], {"blk_2": lax.rem(z + 1, 8)})
+    line.wait_recv()
+
+    def block(back):
+        return all_ref.at[core, outer, lax.rem(inner + 4 - back, 4)]
+
+    def inward(step):
+        src = block(0)
+        return remote(src, src, in_send.at[step - 1], in_recv.at[step - 1], plane_id(step, 0))
+
+    def outward(back, step):
+        src = block(back)
+        return remote(src, src, out_send.at[back, step - 1], out_recv.at[back, step - 1], plane_id(0, step))
+
+    for step in NEAR:
+        inward(step).start()
+    for step in NEAR:
+        outward(0, step).start()
+    for back in NEAR:
+        inward(back).wait_recv()
+        for step in NEAR:
+            outward(back, step).start()
+
+    def across(back):
+        src = all_ref.at[core, lax.rem(outer + 4 - back, 4)]
+        return remote(src, src, core_send.at[back], core_recv.at[back], {"chan_1": 1 - core})
+
+    across(0).start()
+    for step in NEAR:
+        for back in (0,) + NEAR:
+            outward(back, step).wait_recv()
+        across(step).start()
+
+    for step in range(4):
+        across(step).wait_recv()
     keep_rows.wait()
     keep_ints.wait()
     for buf, k in ((got_rows, 0), (got_ints, 1)):
         span = buf.at[pl.ds(0, NT - 1)]
-        pltpu.make_async_remote_copy(
-            src_ref=span, dst_ref=span, send_sem=a2a_send.at[k],
-            recv_sem=a2a_recv.at[k], device_id=other, device_id_type=MESH,
-        ).wait()
-
-
-def exchange(pq, rows, ints):
+        remote(span, span, a2a_send.at[k], a2a_recv.at[k], {"chan_1": 1 - core}).wait()
+    for step in range(1, 4):
+        piece(step).wait_send()
+        inward(step).wait_send()
+        for back in range(4):
+            outward(back, step).wait_send()
+    line.wait_send()
+    for step in range(4):
+        across(step).wait_send()
+
+
+CUT = (28, 52)
+
+
+def front(pm, vis, mod, flag, index, codes):
+    dma = pltpu.SemaphoreType.DMA
     return pl.pallas_call(
-        exchange_kernel,
-        name="exchange",
+        front_kernel,
+        name="front",
         out_shape=(
             jax.ShapeDtypeStruct((2, 4, 4, 8, 16, 128), BF16),
             jax.ShapeDtypeStruct((NT, 8, 128), BF16),
             jax.ShapeDtypeStruct((NT, 4, 128), I32),
         ),
-        in_specs=[VM, VM, VM],
+        in_specs=[SM, VM, VM, VM, VM, VM],
         out_specs=(VM, VM, VM),
         scratch_shapes=[
+            pltpu.VMEM((512, 256), BF16),
+            pltpu.VMEM((256, 256), BF16),
+            pltpu.VMEM((4, 8, 256), F32),
+            pltpu.VMEM((NT, 8, 128), BF16),
+            pltpu.VMEM((NT, 4, 128), I32),
             pltpu.VMEM((3, 8, 256), F32),
-            pltpu.SemaphoreType.DMA((7,)),
-            pltpu.SemaphoreType.DMA((7,)),
-            pltpu.SemaphoreType.DMA((2,)),
-            pltpu.SemaphoreType.DMA((2,)),
-            pltpu.SemaphoreType.DMA((2,)),
+            dma((3,)), dma((3,)), dma((1,)), dma((1,)), dma((3,)), dma((3,)), dma((4, 3)), dma((4, 3)),
+            dma((4,)), dma((4,)), dma((2,)), dma((2,)), dma((2,)),
         ],
         compiler_params=pltpu.CompilerParams(collective_id=0, has_side_effects=True),
-    )(pq, rows, ints)
-
-
-def solve(wide_ref, gain_ref, p_refs):
-    def lines(core, xl, half, slot, part):
-        out = []
-        for xh in range(2):
-            group = core * 4 + xh * 2 + xl
-            out.append(wide_ref[pl.ds(group * 512 + half * 8 + slot * 3 + part, 32, stride=16), :])
-        return out
-
+    )(pm, vis, mod, flag, index, codes)
+
+
+def wide_lines(wide_ref, core, xl, row):
+    out = []
+    for xh in range(2):
+        for y in range(4):
+            x = xh * 2 + xl
+            place = (x * 4 + y) if core == 0 else (16 + y * 4 + x)
+            out.append(wide_ref[pl.ds(place * 128 + row, 8, stride=16), :])
+    return out
+
+
+def block_row(block):
+    n = block.astype(I32)
+    return ((n & 3) << 2) | (n >> 2)
+
+
+def start_gains(amp_ref, phase_ref):
+    amp, phase = amp_ref[...], phase_ref[...]
+    out = []
+    for value in (amp * jnp.cos(phase), amp * jnp.sin(phase)):
+        stacked = jnp.concatenate([value[:, a * 32 : a * 32 + 32] for a in range(4)], axis=0)
+        stacked = jnp.concatenate([stacked, jnp.zeros((112, 32), F32)], axis=0)
+        out.append(stacked.T)
+    return out
+
+
+def solve(wide_ref, amp_ref, phase_ref, p_refs):
     for core in range(2):
         for xl in range(2):
             for half in range(2):
                 tb = (xl * 2 + core) * 2 + half
                 for part in range(3):
-                    block = lines(core, xl, half, 0, part) + lines(core, xl, half, 1, part)
+                    block = []
+                    for slot in range(2):
+                        block += wide_lines(wide_ref, core, xl, half * 8 + slot * 3 + part)
                     p_refs[part][tb * 128 : tb * 128 + 128, :] = jnp.concatenate(block, axis=0).T
 
-    def pair_lines(side):
-        out = []
+    lane = iota((128, 128), 1)
+    columns = []
+    for side in range(2):
+        block = []
         for slot in range(2):
-            for xh in range(2):
-                out.append(wide_ref[pl.ds((xh * 2) * 512 + slot * 8 + 6 + side, 32, stride=16), :])
-        return out
-
-    lane = iota((128, 128), 1).astype(F32)
-    blocks = [pair_lines(0), pair_lines(1)]
-    columns = [jnp.concatenate(b, axis=0) for b in blocks]
+            block += wide_lines(wide_ref, 0, 0, slot * 8 + 6 + side)
+        columns.append(block_row(jnp.concatenate(block, axis=0)))
     onehot = jnp.concatenate([(c == lane).astype(F32) for c in columns], axis=0)
-    rows = [c.T[:32].astype(I32) for c in columns]
+    rows = [c.astype(F32).T[:32].astype(I32) for c in columns]
 
     def spread(g, which):
         return jnp.take_along_axis(g, rows[which], axis=1)
 
     pr_ref, pi_ref, q_ref = p_refs
-    gr = gain_ref[0]
-    gi = gain_ref[1]
+    gr, gi = start_gains(amp_ref, phase_ref)
     for sweep in range(ITERS):
         ar, ai, br, bi = spread(gr, 0), spread(gi, 0), spread(gr, 1), spread(gi, 1)
         a2 = ar * ar + ai * ai
@@ -319,16 +373,14 @@
     turned_i = jnp.concatenate([turned_i] * 4, axis=1)
 
     def blocks(slot, side):
-        return jnp.concatenate(
-            [wide_ref[pl.ds((xh * 2) * 512 + slot * 8 + 6 + side, 32, stride=16), :] for xh in range(2)], axis=0
-        )
+        return block_row(jnp.concatenate(wide_lines(wide_ref, 0, 0, slot * 8 + 6 + side), axis=0))
 
     lane = iota((NT, 128), 1)
     which = jnp.where(
         lane < 64,
         jnp.where(lane < 32, blocks(0, 0), blocks(1, 0)),
         jnp.where(lane < 96, blocks(0, 1), blocks(1, 1)),
-    ).astype(I32)
+    )
     table_r = jnp.zeros((NT, 128), F32)
     table_i = jnp.zeros((NT, 128), F32)
     for n in range(NB):
@@ -364,12 +416,14 @@
     return block, value
 
 
-def owner_kernel(all_ref, rows_ref, ints_ref, gain_ref, grid_ref, solved_ref, wide_ref, pr_ref, pi_ref, q_ref, lines_ref, res_ref):
+def owner_kernel(all_ref, rows_ref, ints_ref, amp_ref, phase_ref, grid_ref, solved_ref, wide_ref, pr_ref, pi_ref, q_ref, lines_ref, res_ref):
     wide_ref[...] = all_ref[...].astype(F32)
     lines_ref[...] = rows_ref[...].astype(F32)
-    gr, gi = solve(wide_ref, gain_ref, (pr_ref, pi_ref, q_ref))
-    solved_ref[0] = gr.T[:NB, :]
-    solved_ref[1] = gi.T[:NB, :]
+    gr, gi = solve(wide_ref, amp_ref, phase_ref, (pr_ref, pi_ref, q_ref))
+    for part, g in enumerate((gr, gi)):
+        turned = g.T
+        at = [(n % 4) * 4 + n // 4 for n in range(NB)]
+        solved_ref[part : part + 1, :] = jnp.concatenate([turned[n : n + 1, :] for n in at], axis=1)
     residual_rows(gr, gi, wide_ref, lines_ref, ints_ref, res_ref)
 
     def step(group, acc):
@@ -400,15 +454,15 @@
     grid_ref[1] = acc[:, TS:]
 
 
-def owner(everything, rows, ints, gains):
+def owner(everything, rows, ints, amp, phase):
     return pl.pallas_call(
         owner_kernel,
         name="owner",
         out_shape=(
             jax.ShapeDtypeStruct((2, TS, TS), F32),
-            jax.ShapeDtypeStruct((2, NB, BS), F32),
+            jax.ShapeDtypeStruct((2, S), F32),
         ),
-        in_specs=[VM, VM, VM, VM],
+        in_specs=[VM] * 5,
         out_specs=(VM, VM),
         scratch_shapes=[
             pltpu.VMEM((4096, 128), F32),
@@ -418,23 +472,15 @@
             pltpu.VMEM((512, 128), F32),
             pltpu.VMEM((2, 2, NT, 128), F32),
         ],
-    )(everything.reshape(4096, 128), rows.reshape(512, 128), ints.reshape(256, 128), gains)
-
-
-def start_gains(gain_amp, gain_phase):
-    both = jnp.stack((gain_amp * jnp.cos(gain_phase), gain_amp * jnp.sin(gain_phase)))
-    turned = both.reshape(2, NB, BS).transpose(0, 2, 1)
-    return jnp.pad(turned, ((0, 0), (0, 0), (0, 128 - NB)))
+    )(everything.reshape(4096, 128), rows.reshape(512, 128), ints.reshape(256, 128), amp.reshape(4, 128), phase.reshape(4, 128))
 
 
 def shards(pair_map, visibilities, model_vis, flag_mask, gain_amp, gain_phase, row_index, cell_codes):
-    gains = start_gains(gain_amp, gain_phase)
-    pq, rows, ints = sender(
+    everything, got_rows, got_ints = front(
         pair_map, visibilities, model_vis, flag_mask, row_index[0, 0], cell_codes.reshape(2, NT, 256)
     )
-    everything, got_rows, got_ints = exchange(pq, rows, ints)
-    grid, solved = owner(everything, got_rows, got_ints, gains)
-    return grid[None, None], solved.reshape(2, S)
+    grid, solved = owner(everything, got_rows, got_ints, gain_amp, gain_phase)
+    return grid[None, None], solved
 
 
 def solution(mesh):

time: 71.1 us -> 49.1 us (0.69)
  Pallas kernels: 67.1 us -> 48.4 us
  local copies, waits for them, and re-layouts: 3 us -> 0 us
    pallas_call x2 -> x1, Pallas kernels: 55.1 us -> 36.2 us  [front(): pl.pallas_call(front_kernel, name='front', out_shape=(jax.ShapeDtypeStruc...]
    reshape x1 -> x0, local copies, waits for them, and re-layouts: 1.39 us -> none  [shards(): return (grid[None, None], solved.reshape(2, S))]
where the time goes in v2:
time: 49.1 us; the launch traced here: 49 us
  Pallas kernels  48.4 us (99%)
  between operations  0.64 us (1%)
    pallas_call x1, Pallas kernels, front(): pl.pallas_call(front_kernel, name='front', out_shape=(jax.ShapeDtypeStruc...  36.2 us
    pallas_call x1, Pallas kernels, owner(): pl.pallas_call(owner_kernel, name='owner', out_shape=(jax.ShapeDtypeStruc...  12.2 us

profile of v2, /device:TPU:1, one launch (start us, length us, event | category | flops | bytes accessed | tf_op | source)
XLA Modules:
  0.0 49.0 jit_solution(4229751952096697853)
XLA Ops:
  0.6 36.2 %front.1 = (bf16[2,4,4,8,16,128]{5,4,3,2,1,0:T(8,128)(2,1)}, bf16[64,8,128]{2,1,0:T(8,128)(2,1)}, s32[64,4,128]{2,1,0:T(4,128)}) custom-call(s32[2,2]{1,0:T(2,128)} %pm_ref.1, bf16[2,2,16,1024]{3,2,1,0:T(8,128)(2,1)} %vis_ref.1, bf16[2,2,16,1024]{3,2,1,0:T(8,128)(2,1)} %mod_ref.1, s32[2,16,1024]{2,1,0:T(8,128)} %flag_ref.1, s32[64,256]{1,0:T(8,128)} %bitcast.12, ...), custom_call_target="tpu_custom_call" | custom-call | tf_op jit(solution)/shard_map/front/pallas_call | solution.py:260
  36.8 12.2 %owner.1 = (f32[2,128,128]{2,1,0:T(8,128)}, f32[2,512]{1,0:T(2,128)}) custom-call(bf16[4096,128]{1,0:T(8,128)(2,1)} %bitcast.8, bf16[512,128]{1,0:T(8,128)(2,1)} %bitcast.9, s32[256,128]{1,0:T(8,128)} %bitcast.10, f32[4,128]{1,0:T(4,128)} %bitcast.13, f32[4,128]{1,0:T(4,128)} %bitcast.14), custom_call_target="tpu_custom_call" | custom-call | tf_op jit(solution)/shard_map/owner/pallas_call | solution.py:458

commit v3 on v2

v3 whole, which is shorter than its diff:
```python
import math

import jax
import jax.numpy as jnp
from jax import lax
from jax.experimental import pallas as pl
from jax.experimental.pallas import tpu as pltpu
from jax.sharding import Mesh
from jax.sharding import PartitionSpec as P

S = 512
BS = 32
NB = 16
ITERS = 3
TS = 128
NT = 64
CH = 16
F32 = jnp.float32
BF16 = jnp.bfloat16
I32 = jnp.int32
MESH = pl.DeviceIdType.MESH
BLK = ("blk_0", "blk_1", "blk_2")
CHAN = ("chan_0", "chan_1")
VM = pl.BlockSpec(memory_space=pltpu.VMEM)
SM = pl.BlockSpec(memory_space=pltpu.SMEM)


def iota(shape, axis):
    return lax.broadcasted_iota(I32, shape, axis)


def sums_and_tables(pm_ref, vis_ref, mod_ref, flag_ref, pq_ref, table_ref):
    for slot in range(2):
        first = pm_ref[slot, 0]
        second = pm_ref[slot, 1]
        same = (first == second).astype(F32)
        lane = iota((1, 128), 1)
        planes = [[], [], [], []]
        for tb in range(8):
            at = slice(tb * 128, tb * 128 + 128)
            base = lane + tb * 128
            diagonal = ((base >> 5) == (base & 31)).astype(F32)
            weight = flag_ref[slot, :, at].astype(F32) * (1.0 - same * diagonal)
            vr = vis_ref[0, slot, :, at].astype(F32) * weight
            vi = vis_ref[1, slot, :, at].astype(F32) * weight
            mr = mod_ref[0, slot, :, at].astype(F32) * weight
            mi = mod_ref[1, slot, :, at].astype(F32) * weight
            sums = (
                jnp.sum(vr * mr + vi * mi, axis=0, keepdims=True),
                jnp.sum(vi * mr - vr * mi, axis=0, keepdims=True),
                jnp.sum(mr * mr + mi * mi, axis=0, keepdims=True),
            )
            col = slice((tb % 2) * 128, (tb % 2) * 128 + 128)
            for q in range(3):
                row = slot * 3 + q
                pq_ref[tb // 2, row : row + 1, col] = sums[q]
            for plane, value in zip(planes, (vr, vi, mr, mi)):
                plane.append(value)
        for q in range(4):
            table = jnp.concatenate(planes[q], axis=0)
            table_ref[q * 128 : q * 128 + 128, slot * 128 : slot * 128 + 128] = table.T.astype(BF16)
        for quarter in range(4):
            col = slice(slot * 128, slot * 128 + 128)
            pq_ref[quarter, 6:7, col] = jnp.full((1, 128), first.astype(F32))
            pq_ref[quarter, 7:8, col] = jnp.full((1, 128), second.astype(F32))


def iota_table():
    return iota((256, 256), 0).astype(F32).astype(BF16)


def gather_tile(tile, index_ref, codes_ref, table_ref, iota_ref, rows_ref):
    index = index_ref[pl.ds(tile, 1), :]
    hi = ((index >> 14) << 7) | (((index >> 7) & 7) << 4) | ((index >> 10) & 15)
    high = jnp.broadcast_to(hi.astype(F32), (16, 256)).astype(BF16)
    one, zero = jnp.ones((16, 256), BF16), jnp.zeros((16, 256), BF16)
    onehot = jnp.concatenate(
        [jnp.where(iota_ref[k * 16 : k * 16 + 16, :] == high, one, zero) for k in range(16)], axis=0
    )
    lifted = jnp.dot(table_ref[...], onehot, preferred_element_type=F32)
    low_high = (index >> 3) & 15
    live = iota((8, 256), 0) == (index & 7)
    masks = [jnp.broadcast_to(low_high == k, (8, 256)) for k in range(16)]
    pieces = []
    for q in range(4):
        part = lifted[q * 128 : q * 128 + 8]
        for k in range(1, 16):
            part = jnp.where(masks[k], lifted[q * 128 + k * 8 : q * 128 + k * 8 + 8], part)
        value = jnp.sum(jnp.where(live, part, 0.0), axis=0, keepdims=True)
        pieces += [value[:, :128], value[:, 128:]]
    rows_ref[tile] = jnp.concatenate(pieces, axis=0).astype(BF16)


def write_ints(tile, index_ref, codes_ref, ints_ref):
    index = index_ref[pl.ds(tile, 1), :]
    both = codes_ref[0, pl.ds(tile, 1), :] | (codes_ref[1, pl.ds(tile, 1), :] << 16)
    place = (((index >> 14) & 1) << 10) | (index & 1023)
    ints_ref[tile] = jnp.concatenate([both[:, :128], both[:, 128:], place[:, :128], place[:, 128:]], axis=0)


def widen(all_ref, wide_ref, core):
    wide_ref[pl.ds(pl.multiple_of(core * 2048, 2048), 2048), :] = all_ref[core].astype(F32).reshape(2048, 128)


def wide_lines(wide_ref, core, xl, row):
    out = []
    for xh in range(2):
        for y in range(4):
            x = xh * 2 + xl
            place = core * 16 + (x * 4 + y) * (1 - core) + (y * 4 + x) * core
            out.append(wide_ref[pl.ds(place * 128 + row, 8, stride=16), :])
    return out


def turn(wide_ref, core, p_refs):
    for xl in range(2):
        for half in range(2):
            tb = (xl * 2 + core) * 2 + half
            for part in range(3):
                block = []
                for slot in range(2):
                    block += wide_lines(wide_ref, core, xl, half * 8 + slot * 3 + part)
                at = pl.ds(pl.multiple_of(tb * 128, 128), 128)
                p_refs[part][at, :] = jnp.concatenate(block, axis=0).T


def block_row(block):
    n = block.astype(I32)
    return ((n & 3) << 2) | (n >> 2)


def station_maps(wide_ref, core):
    found = []
    for side in range(2):
        for slot in range(2):
            found.append(block_row(jnp.concatenate(wide_lines(wide_ref, core, 0, slot * 8 + 6 + side), axis=0)))
    lane = iota((128, 128), 1)
    columns = [jnp.concatenate(found[:2], axis=0), jnp.concatenate(found[2:], axis=0)]
    onehot = jnp.concatenate([(c == lane).astype(F32) for c in columns], axis=0)
    rows = [c.astype(F32).T[:32].astype(I32) for c in columns]
    lane = iota((NT, 128), 1)
    which = jnp.where(
        lane < 64, jnp.where(lane < 32, found[0], found[1]), jnp.where(lane < 96, found[2], found[3])
    )
    return onehot, rows, which


def start_gains(amp_ref, phase_ref):
    amp, phase = amp_ref[...], phase_ref[...]
    out = []
    for value in (amp * jnp.cos(phase), amp * jnp.sin(phase)):
        stacked = jnp.concatenate([value[:, a * 32 : a * 32 + 32] for a in range(4)], axis=0)
        stacked = jnp.concatenate([stacked, jnp.zeros((112, 32), F32)], axis=0)
        out.append(stacked.T)
    return out


def solve(gr, gi, onehot, rows, p_refs):
    def spread(g, which):
        return jnp.take_along_axis(g, rows[which], axis=1)

    pr_ref, pi_ref, q_ref = p_refs
    for sweep in range(ITERS):
        ar, ai, br, bi = spread(gr, 0), spread(gi, 0), spread(gr, 1), spread(gi, 1)
        a2 = ar * ar + ai * ai
        b2 = br * br + bi * bi
        zero = jnp.zeros((32, 128), F32)
        first = [zero, zero, zero]
        second = [zero, zero, zero]
        for i in range(32):
            pr = pr_ref[i * 32 : i * 32 + 32, :]
            pi = pi_ref[i * 32 : i * 32 + 32, :]
            q = q_ref[i * 32 : i * 32 + 32, :]
            xr, xi, x2 = ar[i : i + 1], ai[i : i + 1], a2[i : i + 1]
            second[0] = second[0] + (pr * xr + pi * xi)
            second[1] = second[1] + (pr * xi - pi * xr)
            second[2] = second[2] + q * x2
        for j in range(32):
            at = pl.ds(j, 32, stride=32)
            pr, pi, q = pr_ref[at, :], pi_ref[at, :], q_ref[at, :]
            xr, xi, x2 = br[j : j + 1], bi[j : j + 1], b2[j : j + 1]
            first[0] = first[0] + (pr * xr - pi * xi)
            first[1] = first[1] + (pr * xi + pi * xr)
            first[2] = first[2] + q * x2
        terms = jnp.concatenate([jnp.concatenate(first, axis=0), jnp.concatenate(second, axis=0)], axis=1)
        total = jnp.dot(terms, onehot, precision=lax.Precision.HIGHEST, preferred_element_type=F32)
        denominator = jnp.where(iota((32, 128), 1) < NB, total[64:96], 1.0)
        ur = total[0:32] / denominator
        ui = total[32:64] / denominator
        if sweep % 2 == 1:
            gr, gi = 0.5 * (ur + gr), 0.5 * (ui + gi)
        else:
            gr, gi = ur, ui
    return gr, gi


def residual_rows(gr, gi, which, lines_ref, ints_ref, res_ref):
    turned_r = gr.T[:NB, :]
    turned_i = gi.T[:NB, :]
    turned_r = jnp.concatenate([turned_r] * 4, axis=1)
    turned_i = jnp.concatenate([turned_i] * 4, axis=1)

    table_r = jnp.zeros((NT, 128), F32)
    table_i = jnp.zeros((NT, 128), F32)
    for n in range(NB):
        hit = which == n
        table_r = jnp.where(hit, turned_r[n : n + 1], table_r)
        table_i = jnp.where(hit, turned_i[n : n + 1], table_i)
    for half in range(2):
        place = ints_ref[:, 2 + half, :]
        slot = (place >> 10) * 32
        at_a = slot + ((place >> 5) & 31)
        at_b = slot + (place & 31) + 64
        ar = jnp.take_along_axis(table_r, at_a, axis=1)
        ai = jnp.take_along_axis(table_i, at_a, axis=1)
        br = jnp.take_along_axis(table_r, at_b, axis=1)
        bi = jnp.take_along_axis(table_i, at_b, axis=1)
        vr, vi, mr, mi = (lines_ref[pl.ds(q * 2 + half, NT, stride=8), :] for q in range(4))
        twisted_r = mr * br + mi * bi
        twisted_i = mi * br - mr * bi
        res_ref[0, half] = (vr - (ar * twisted_r - ai * twisted_i)).astype(BF16).astype(F32)
        res_ref[1, half] = (vi - (ar * twisted_i + ai * twisted_r)).astype(BF16).astype(F32)


def window(code):
    shifted = iota((8, 128), 0) * 8 - code
    block = (32 - shifted) >> 6
    distance = block * 64 + shifted
    angle = distance.astype(F32) * (math.pi / 64)
    z = angle * angle
    cos = 1.0 / math.factorial(14)
    for k in range(6, -1, -1):
        cos = 1.0 / math.factorial(2 * k) - z * cos
    value = jnp.where(jnp.abs(distance) < 32, cos * cos, 0.0).astype(BF16).astype(F32)
    return block, value


NEAR = (1, 3, 2)
SLOT = (0, 1, 3, 5, 7, 6, 4, 2)
GROUPS = ((0, 5), (5, 3))
CUT = (20, 36, 48)


def kernel(
    pm_ref, vis_ref, mod_ref, flag_ref, index_ref, codes_ref, amp_ref, phase_ref,
    grid_ref, solved_ref,
    table_ref, iota_ref, pq_ref, rows_ref, ints_ref, part, all_ref, got_rows, got_ints,
    wide_ref, pr_ref, pi_ref, q_ref, lines_ref, res_ref, left_ref, vblock_ref, vvalue_ref,
    sum_send, sum_recv, line_send, line_recv, in_send, in_recv, out_send, out_recv,
    core_send, core_recv, a2a_send, a2a_recv, own_sem, plane_sem, far_sem,
):
    xh, y, z = lax.axis_index("blk_0"), lax.axis_index("blk_1"), lax.axis_index("blk_2")
    xl, core = lax.axis_index("chan_0"), lax.axis_index("chan_1")
    me = xh * 4 + y
    x = xh * 2 + xl
    quarter = xl * 2 + core
    inner = y * (1 - core) + x * core
    outer = x * (1 - core) + y * core

    def chan_id(step):
        c = lax.rem(quarter + step, 4)
        return c, {"chan_0": c // 2, "chan_1": lax.rem(c, 2)}

    def line_id(step):
        return {"blk_2": lax.rem(z + step, 8)}

    def y_id(step):
        return {"blk_1": lax.rem(y + step, 4)}

    def x_id(step):
        return {"blk_0": lax.rem(x + step, 4) // 2, "chan_0": lax.rem(x + step, 2)}

    def plane_id(in_step, out_step):
        i, o = lax.rem(inner + in_step, 4), lax.rem(outer + out_step, 4)
        py = i * (1 - core) + o * core
        px = o * (1 - core) + i * core
        return {"blk_0": px // 2, "chan_0": lax.rem(px, 2), "blk_1": py}

    def signal(sem, device):
        pl.semaphore_signal(sem, inc=1, device_id=device, device_id_type=MESH)

    barrier = pltpu.get_barrier_semaphore()
    for step in range(1, 4):
        signal(barrier, chan_id(step)[1])
        signal(barrier, x_id(step))
        signal(barrier, y_id(step))
    for step in range(1, 8):
        signal(barrier, line_id(step))

    def remote(src, dst, send, recv, device):
        return pltpu.make_async_remote_copy(
            src_ref=src, dst_ref=dst, send_sem=send, recv_sem=recv, device_id=device, device_id_type=MESH
        )

    def gather(first, last):
        def step(group, carry):
            for member in range(4):
                gather_tile(group * 4 + member, index_ref, codes_ref, table_ref, iota_ref, rows_ref)
            return carry

        lax.fori_loop(first // 4, last // 4, step, 0)

    def to_owners(src, dst, k):
        for away in range(8):
            tz = lax.rem(z + away, 8)
            slot = SLOT[(8 - away) % 8]

            def step(n, carry):
                line = lax.rem(me + n, 8)
                device = {"blk_0": line // 4, "blk_1": lax.rem(line, 4), "blk_2": tz}
                remote(src.at[line * 8 + tz], dst.at[me * 8 + slot], a2a_send.at[k], a2a_recv.at[k], device).start()
                return carry

            lax.fori_loop(1 if away == 0 else 0, 8, step, 0)
        keep = pltpu.make_async_copy(src.at[me * 8 + z], dst.at[me * 8], own_sem.at[k])
        keep.start()
        return keep

    def owners_done(buf, k, keep):
        span = buf.at[pl.ds(0, NT - 1)]
        remote(span, span, a2a_send.at[k], a2a_recv.at[k], {"chan_1": 1 - core}).wait()
        keep.wait()

    sums_and_tables(pm_ref, vis_ref, mod_ref, flag_ref, pq_ref, table_ref)
    pl.semaphore_wait(barrier, 16)
    for step in range(1, 4):
        signal(plane_sem, y_id(step))

    def piece(step):
        c, device = chan_id(step)
        return remote(pq_ref.at[c], part.at[step - 1], sum_send.at[step - 1], sum_recv.at[step - 1], device)

    for step in range(1, 4):
        piece(step).start()
    iota_ref[...] = iota_table()

    def ints_step(group, carry):
        for member in range(4):
            write_ints(group * 4 + member, index_ref, codes_ref, ints_ref)
        return carry

    lax.fori_loop(0, NT // 4, ints_step, 0)
    gather(0, CUT[0])
    total = pq_ref[quarter]
    for step in range(1, 4):
        piece(step).wait_recv()
        total = total + part[step - 1]
    total = jnp.concatenate([total[:6], pq_ref[0, 6:8, :]], axis=0)
    all_ref[core, outer, inner, 0] = jnp.concatenate([total[:, :128], total[:, 128:]], axis=0).astype(BF16)

    mine = all_ref.at[core, outer, inner, 0]

    def along(step):
        slot = SLOT[(8 - step) % 8]
        k = 0 if slot < 5 else 1
        return remote(mine, all_ref.at[core, outer, inner, slot], line_send.at[k], line_recv.at[k], line_id(step))

    for step in (1, 7, 2, 6, 3, 5, 4):
        along(step).start()
    pl.semaphore_wait(plane_sem, 3)
    signal(far_sem, {"blk_0": 1 - xh})
    pl.semaphore_wait(far_sem, 1)
    keep_ints = to_owners(ints_ref, got_ints, 1)
    gather(CUT[0], CUT[1])

    def line(k):
        count = (4, 3)[k]
        span = all_ref.at[core, outer, inner, pl.ds(0, count)]
        return remote(span, span, line_send.at[k], line_recv.at[k], line_id(1))

    def block(back, k):
        return all_ref.at[core, outer, lax.rem(inner + 4 - back, 4), pl.ds(*GROUPS[k])]

    def inward(step, k):
        src = block(0, k)
        return remote(src, src, in_send.at[k, step - 1], in_recv.at[k, step - 1], plane_id(step, 0))

    def outward(back, step, k):
        src = block(back, k)
        return remote(src, src, out_send.at[k, back, step - 1], out_recv.at[k, back, step - 1], plane_id(0, step))

    for k in range(2):
        line(k).wait_recv()
        for step in NEAR:
            inward(step, k).start()
        for step in NEAR:
            outward(0, step, k).start()
        if k == 0:
            gather(CUT[1], CUT[2])
    gather(CUT[2], NT)
    for k in range(2):
        for back in NEAR:
            inward(back, k).wait_recv()
            for step in NEAR:
                outward(back, step, k).start()
    keep_rows = to_owners(rows_ref, got_rows, 0)

    owners_done(got_ints, 1, keep_ints)

    def windows(s, carry):
        for half in range(2):
            both = got_ints[s, half : half + 1, :]
            ublock, uvalue = window(both & 65535)
            vblock, vvalue = window(both >> 16)
            at = pl.ds(pl.multiple_of((s * 2 + half) * 8, 8), 8)
            vblock_ref[at, :] = vblock
            vvalue_ref[at, :] = vvalue
            left_ref[:, pl.ds(pl.multiple_of((s * 2 + half) * 128, 128), 128)] = jnp.concatenate(
                [jnp.where(ublock == k, uvalue, 0.0) for k in range(16)], axis=0
            ).astype(BF16)
        return carry

    lax.fori_loop(0, NT, windows, 0)
    gr, gi = start_gains(amp_ref, phase_ref)

    def across(back):
        src = all_ref.at[core, lax.rem(outer + 4 - back, 4)]
        return remote(src, src, core_send.at[back], core_recv.at[back], {"chan_1": 1 - core})

    across(0).start()
    for step in NEAR:
        for k in range(2):
            for back in (0,) + NEAR:
                outward(back, step, k).wait_recv()
        across(step).start()

    p_refs = (pr_ref, pi_ref, q_ref)
    widen(all_ref, wide_ref, core)
    turn(wide_ref, core, p_refs)
    onehot, rows, which = station_maps(wide_ref, core)
    for step in range(4):
        across(step).wait_recv()
    widen(all_ref, wide_ref, 1 - core)
    turn(wide_ref, 1 - core, p_refs)
    gr, gi = solve(gr, gi, onehot, rows, p_refs)
    for part_at, g in enumerate((gr, gi)):
        turned = g.T
        at = [(n % 4) * 4 + n // 4 for n in range(NB)]
        solved_ref[part_at : part_at + 1, :] = jnp.concatenate([turned[n : n + 1, :] for n in at], axis=1)

    owners_done(got_rows, 0, keep_rows)
    lines_ref[...] = got_rows[...].astype(F32).reshape(512, 128)
    residual_rows(gr, gi, which, lines_ref, got_ints, res_ref)

    def grid_step(group, acc):
        rights = []
        for member in range(4):
            s = group * 4 + member
            for half in range(2):
                at = pl.ds(pl.multiple_of((s * 2 + half) * 8, 8), 8)
                vblock, vvalue = vblock_ref[at, :], vvalue_ref[at, :]
                hr = vvalue * res_ref[0, half, pl.ds(s, 1), :]
                hi = vvalue * res_ref[1, half, pl.ds(s, 1), :]
                hits = [vblock == k for k in range(16)]
                rights.append(
                    jnp.concatenate(
                        [jnp.where(hit, hr, 0.0) for hit in hits] + [jnp.where(hit, hi, 0.0) for hit in hits], axis=0
                    ).astype(BF16)
                )
        left = left_ref[:, pl.ds(pl.multiple_of(group * 1024, 1024), 1024)]
        right = jnp.concatenate(rights, axis=1)
        return acc + lax.dot_general(left, right, (((1,), (1,)), ((), ())), preferred_element_type=F32)

    acc = lax.fori_loop(0, NT // 4, grid_step, jnp.zeros((TS, 2 * TS), F32))
    grid_ref[0] = acc[:, :TS]
    grid_ref[1] = acc[:, TS:]

    for k in range(2):
        line(k).wait_send()
        for step in range(1, 4):
            inward(step, k).wait_send()
            for back in range(4):
                outward(back, step, k).wait_send()
    for step in range(1, 4):
        piece(step).wait_send()
    for step in range(4):
        across(step).wait_send()


def whole(*operands):
    dma, regular = pltpu.SemaphoreType.DMA, pltpu.SemaphoreType.REGULAR
    return pl.pallas_call(
        kernel,
        name="whole",
        out_shape=(
            jax.ShapeDtypeStruct((2, TS, TS), F32),
            jax.ShapeDtypeStruct((2, S), F32),
        ),
        in_specs=[SM] + [VM] * 7,
        out_specs=(VM, VM),
        scratch_shapes=[
            pltpu.VMEM((512, 256), BF16),
            pltpu.VMEM((256, 256), BF16),
            pltpu.VMEM((4, 8, 256), F32),
            pltpu.VMEM((NT, 8, 128), BF16),
            pltpu.VMEM((NT, 4, 128), I32),
            pltpu.VMEM((3, 8, 256), F32),
            pltpu.VMEM((2, 4, 4, 8, 16, 128), BF16),
            pltpu.VMEM((NT, 8, 128), BF16),
            pltpu.VMEM((NT, 4, 128), I32),
            pltpu.VMEM((4096, 128), F32),
            pltpu.VMEM((1024, 128), F32),
            pltpu.VMEM((1024, 128), F32),
            pltpu.VMEM((1024, 128), F32),
            pltpu.VMEM((512, 128), F32),
            pltpu.VMEM((2, 2, NT, 128), F32),
            pltpu.VMEM((TS, NT * 256), BF16),
            pltpu.VMEM((NT * 16, 128), I32),
            pltpu.VMEM((NT * 16, 128), F32),
            dma((3,)), dma((3,)), dma((2,)), dma((2,)), dma((2, 3)), dma((2, 3)), dma((2, 4, 3)), dma((2, 4, 3)),
            dma((4,)), dma((4,)), dma((2,)), dma((2,)), dma((2,)), regular, regular,
        ],
        compiler_params=pltpu.CompilerParams(collective_id=0, has_side_effects=True),
    )(*operands)


def shards(pair_map, visibilities, model_vis, flag_mask, gain_amp, gain_phase, row_index, cell_codes):
    grid, solved = whole(
        pair_map, visibilities, model_vis, flag_mask, row_index[0, 0], cell_codes.reshape(2, NT, 256),
        gain_amp.reshape(4, 128), gain_phase.reshape(4, 128),
    )
    return grid[None, None], solved


def solution(mesh):
    split = Mesh(mesh.devices.reshape(2, 4, 8, 2, 2), BLK + CHAN)
    placed = (
        P(BLK, None),
        P(None, BLK, CHAN, None),
        P(None, BLK, CHAN, None),
        P(BLK, CHAN, None),
        P(),
        P(),
        P(CHAN, BLK, None, None),
        P(None, CHAN, BLK, None, None),
    )
    return jax.shard_map(
        shards,
        mesh=split,
        in_specs=placed,
        out_specs=(P(CHAN, BLK, None, None, None), P()),
        check_vma=False,
    )
```

time: 49.1 us -> 45.2 us (0.921)
  Pallas kernels: 48.4 us -> 42.3 us
  local copies, waits for them, and re-layouts: 0 us -> 2.17 us
    pallas_call x2 -> x1, Pallas kernels: 48.4 us -> 42.3 us  [whole(): pl.pallas_call(kernel, name='whole', out_shape=(jax.ShapeDtypeStruct((2,...]
    unnamed x0 -> x4, local copies, waits for them, and re-layouts: none -> 2.17 us
where the time goes in v3:
time: 45.2 us; the launch traced here: 45.1 us
  Pallas kernels  42.3 us (94%)
  local copies, waits for them, and re-layouts  2.17 us (5%)
  between operations  0.65 us (1%)
    pallas_call x1, Pallas kernels, whole(): pl.pallas_call(kernel, name='whole', out_shape=(jax.ShapeDtypeStruct((2,...  42.3 us
    unnamed x4, local copies, waits for them, and re-layouts  2.17 us

profile of v3, /device:TPU:1, one launch (start us, length us, event | category | flops | bytes accessed | tf_op | source)
XLA Modules:
  0.0 45.1 jit_solution(3646651386977954584)
XLA Ops:
  0.6 42.3 %whole.1 = (f32[2,128,128]{2,1,0:T(8,128)}, f32[2,512]{1,0:T(2,128)}) custom-call(s32[2,2]{1,0:T(2,128)} %pm_ref.1, bf16[2,2,16,1024]{3,2,1,0:T(8,128)(2,1)} %vis_ref.1, bf16[2,2,16,1024]{3,2,1,0:T(8,128)(2,1)} %mod_ref.1, s32[2,16,1024]{2,1,0:T(8,128)} %flag_ref.1, s32[64,256]{1,0:T(8,128)} %bitcast.7, s32[2,64,256]{2,1,0:T(8,128)} %bitcast.6, ...), custom_call_target="tpu_custom_call" | custom-call | tf_op jit(solution)/shard_map/whole/pallas_call | solution.py:482
  42.9 0.0 copy-start
  42.9 1.6 %copy.12 = f32[1,1,2,128,128]{4,3,2,1,0:T(8,128)} copy(f32[1,1,2,128,128]{4,3,2,1,0:T(8,128)} %bitcast.5) | data formatting | bytes 262144
  44.5 0.0 copy-done
  44.5 0.6 %copy.13 = f32[2,512]{1,0:T(2,128)} copy(f32[2,512]{1,0:T(2,128)S(1)} %copy-done) | data formatting | bytes 8192
Async XLA Ops:
  42.9 1.6 %copy-start = (f32[2,512]{1,0:T(2,128)S(1)}, f32[2,512]{1,0:T(2,128)}, u32[]{:S(2)}) copy-start(f32[2,512]{1,0:T(2,128)} %get-tuple-element.9) | copy-start | bytes 12292

commit v4 on v3

--- a/solution.py
+++ b/solution.py
@@ -136,7 +136,7 @@
             found.append(block_row(jnp.concatenate(wide_lines(wide_ref, core, 0, slot * 8 + 6 + side), axis=0)))
     lane = iota((128, 128), 1)
     columns = [jnp.concatenate(found[:2], axis=0), jnp.concatenate(found[2:], axis=0)]
-    onehot = jnp.concatenate([(c == lane).astype(F32) for c in columns], axis=0)
+    onehot = jnp.concatenate([(c == lane).astype(F32) for c in columns], axis=0).astype(BF16)
     rows = [c.astype(F32).T[:32].astype(I32) for c in columns]
     lane = iota((NT, 128), 1)
     which = jnp.where(
@@ -153,6 +153,15 @@
         stacked = jnp.concatenate([stacked, jnp.zeros((112, 32), F32)], axis=0)
         out.append(stacked.T)
     return out
+
+
+def station_sums(terms, onehot):
+    high = terms.astype(BF16)
+    rest = terms - high.astype(F32)
+    middle = rest.astype(BF16)
+    low = (rest - middle.astype(F32)).astype(BF16)
+    sums = jnp.dot(jnp.concatenate([high, middle, low], axis=0), onehot, preferred_element_type=F32)
+    return sums[:96] + (sums[96:192] + sums[192:])
 
 
 def solve(gr, gi, onehot, rows, p_refs):
@@ -183,7 +192,7 @@
             first[1] = first[1] + (pr * xi + pi * xr)
             first[2] = first[2] + q * x2
         terms = jnp.concatenate([jnp.concatenate(first, axis=0), jnp.concatenate(second, axis=0)], axis=1)
-        total = jnp.dot(terms, onehot, precision=lax.Precision.HIGHEST, preferred_element_type=F32)
+        total = station_sums(terms, onehot)
         denominator = jnp.where(iota((32, 128), 1) < NB, total[64:96], 1.0)
         ur = total[0:32] / denominator
         ui = total[32:64] / denominator
@@ -222,6 +231,20 @@
         res_ref[1, half] = (vi - (ar * twisted_i + ai * twisted_r)).astype(BF16).astype(F32)
 
 
+def doubled(block):
+    return jnp.concatenate([block, block - 1.0], axis=0).astype(BF16)
+
+
+def spread_out(place, values):
+    zero = jnp.zeros((16, 128), BF16)
+    hits = [place == jnp.full((16, 128), 2.0 * k, BF16) for k in range(8)]
+    out = []
+    for value in values:
+        both = jnp.concatenate([value, value], axis=0).astype(BF16)
+        out += [jnp.where(hit, both, zero) for hit in hits]
+    return jnp.concatenate(out, axis=0)
+
+
 def window(code):
     shifted = iota((8, 128), 0) * 8 - code
     block = (32 - shifted) >> 6
@@ -232,13 +255,13 @@
     for k in range(6, -1, -1):
         cos = 1.0 / math.factorial(2 * k) - z * cos
     value = jnp.where(jnp.abs(distance) < 32, cos * cos, 0.0).astype(BF16).astype(F32)
-    return block, value
+    return block.astype(F32), value
 
 
 NEAR = (1, 3, 2)
 SLOT = (0, 1, 3, 5, 7, 6, 4, 2)
 GROUPS = ((0, 5), (5, 3))
-CUT = (20, 36, 48)
+CUT = (16, 28, 40)
 
 
 def kernel(
@@ -397,20 +420,20 @@
 
     owners_done(got_ints, 1, keep_ints)
 
-    def windows(s, carry):
-        for half in range(2):
-            both = got_ints[s, half : half + 1, :]
-            ublock, uvalue = window(both & 65535)
-            vblock, vvalue = window(both >> 16)
-            at = pl.ds(pl.multiple_of((s * 2 + half) * 8, 8), 8)
-            vblock_ref[at, :] = vblock
-            vvalue_ref[at, :] = vvalue
-            left_ref[:, pl.ds(pl.multiple_of((s * 2 + half) * 128, 128), 128)] = jnp.concatenate(
-                [jnp.where(ublock == k, uvalue, 0.0) for k in range(16)], axis=0
-            ).astype(BF16)
+    def windows(group, carry):
+        for member in range(4):
+            s = group * 4 + member
+            for half in range(2):
+                both = got_ints[s, half : half + 1, :]
+                ublock, uvalue = window(both & 65535)
+                vblock, vvalue = window(both >> 16)
+                at = pl.ds(pl.multiple_of((s * 2 + half) * 8, 8), 8)
+                vblock_ref[at, :] = vblock
+                vvalue_ref[at, :] = vvalue
+                left_ref[:, pl.ds(pl.multiple_of((s * 2 + half) * 128, 128), 128)] = spread_out(doubled(ublock), [uvalue])
         return carry
 
-    lax.fori_loop(0, NT, windows, 0)
+    lax.fori_loop(0, NT // 4, windows, 0)
     gr, gi = start_gains(amp_ref, phase_ref)
 
     def across(back):
@@ -442,28 +465,24 @@
     lines_ref[...] = got_rows[...].astype(F32).reshape(512, 128)
     residual_rows(gr, gi, which, lines_ref, got_ints, res_ref)
 
-    def grid_step(group, acc):
-        rights = []
-        for member in range(4):
-            s = group * 4 + member
-            for half in range(2):
-                at = pl.ds(pl.multiple_of((s * 2 + half) * 8, 8), 8)
-                vblock, vvalue = vblock_ref[at, :], vvalue_ref[at, :]
-                hr = vvalue * res_ref[0, half, pl.ds(s, 1), :]
-                hi = vvalue * res_ref[1, half, pl.ds(s, 1), :]
-                hits = [vblock == k for k in range(16)]
-                rights.append(
-                    jnp.concatenate(
-                        [jnp.where(hit, hr, 0.0) for hit in hits] + [jnp.where(hit, hi, 0.0) for hit in hits], axis=0
-                    ).astype(BF16)
-                )
-        left = left_ref[:, pl.ds(pl.multiple_of(group * 1024, 1024), 1024)]
-        right = jnp.concatenate(rights, axis=1)
-        return acc + lax.dot_general(left, right, (((1,), (1,)), ((), ())), preferred_element_type=F32)
-
-    acc = lax.fori_loop(0, NT // 4, grid_step, jnp.zeros((TS, 2 * TS), F32))
-    grid_ref[0] = acc[:, :TS]
-    grid_ref[1] = acc[:, TS:]
+    def half_tile(s, half):
+        at = pl.ds(pl.multiple_of((s * 2 + half) * 8, 8), 8)
+        place, vvalue = doubled(vblock_ref[at, :]), vvalue_ref[at, :]
+        values = [vvalue * res_ref[p, half, pl.ds(s, 1), :] for p in range(2)]
+        return spread_out(place, values)
+
+    def grid_step(step, acc):
+        for piece_at in range(4):
+            group = step * 4 + piece_at
+            members = [half_tile(group * 8 + member, half) for member in range(8) for half in range(2)]
+            left = left_ref[:, pl.ds(pl.multiple_of(group * 2048, 2048), 2048)]
+            right = jnp.concatenate(members, axis=1)
+            acc = acc + lax.dot_general(right, left, (((1,), (1,)), ((), ())), preferred_element_type=F32)
+        return acc
+
+    acc = lax.fori_loop(0, NT // 32, grid_step, jnp.zeros((2 * TS, TS), F32))
+    grid_ref[0] = acc[:TS].T
+    grid_ref[1] = acc[TS:].T
 
     for k in range(2):
         line(k).wait_send()
@@ -505,7 +524,7 @@
             pltpu.VMEM((512, 128), F32),
             pltpu.VMEM((2, 2, NT, 128), F32),
             pltpu.VMEM((TS, NT * 256), BF16),
-            pltpu.VMEM((NT * 16, 128), I32),
+            pltpu.VMEM((NT * 16, 128), F32),
             pltpu.VMEM((NT * 16, 128), F32),
             dma((3,)), dma((3,)), dma((2,)), dma((2,)), dma((2, 3)), dma((2, 3)), dma((2, 4, 3)), dma((2, 4, 3)),
             dma((4,)), dma((4,)), dma((2,)), dma((2,)), dma((2,)), regular, regular,

time: 45.2 us -> 41 us (0.907)
  Pallas kernels: 42.3 us -> 38 us
    pallas_call x1, Pallas kernels: 42.3 us -> 38 us  [whole(): pl.pallas_call(kernel, name='whole', out_shape=(jax.ShapeDtypeStruct((2,...]
where the time goes in v4:
time: 41 us; the launch traced here: 40.8 us
  Pallas kernels  38 us (93%)
  local copies, waits for them, and re-layouts  2.17 us (5%)
  between operations  0.65 us (2%)
    pallas_call x1, Pallas kernels, whole(): pl.pallas_call(kernel, name='whole', out_shape=(jax.ShapeDtypeStruct((2,...  38 us
    unnamed x4, local copies, waits for them, and re-layouts  2.17 us

profile of v4, /device:TPU:1, one launch (start us, length us, event | category | flops | bytes accessed | tf_op | source)
XLA Modules:
  0.0 40.8 jit_solution(12081858444667631435)
XLA Ops:
  0.6 38.0 %whole.1 = (f32[2,128,128]{2,1,0:T(8,128)}, f32[2,512]{1,0:T(2,128)}) custom-call(s32[2,2]{1,0:T(2,128)} %pm_ref.1, bf16[2,2,16,1024]{3,2,1,0:T(8,128)(2,1)} %vis_ref.1, bf16[2,2,16,1024]{3,2,1,0:T(8,128)(2,1)} %mod_ref.1, s32[2,16,1024]{2,1,0:T(8,128)} %flag_ref.1, s32[64,256]{1,0:T(8,128)} %bitcast.7, s32[2,64,256]{2,1,0:T(8,128)} %bitcast.6, ...), custom_call_target="tpu_custom_call" | custom-call | tf_op jit(solution)/shard_map/whole/pallas_call | solution.py:501
  38.7 0.0 copy-start
  38.7 1.6 %copy.12 = f32[1,1,2,128,128]{4,3,2,1,0:T(8,128)} copy(f32[1,1,2,128,128]{4,3,2,1,0:T(8,128)} %bitcast.5) | data formatting | bytes 262144
  40.2 0.0 copy-done
  40.2 0.6 %copy.13 = f32[2,512]{1,0:T(2,128)} copy(f32[2,512]{1,0:T(2,128)S(1)} %copy-done) | data formatting | bytes 8192
Async XLA Ops:
  38.7 1.6 %copy-start = (f32[2,512]{1,0:T(2,128)S(1)}, f32[2,512]{1,0:T(2,128)}, u32[]{:S(2)}) copy-start(f32[2,512]{1,0:T(2,128)} %get-tuple-element.9) | copy-start | bytes 12292

commit v5 on v4

--- a/solution.py
+++ b/solution.py
@@ -29,22 +29,19 @@
     return lax.broadcasted_iota(I32, shape, axis)
 
 
-def sums_and_tables(pm_ref, vis_ref, mod_ref, flag_ref, pq_ref, table_ref):
+def weighted(pm_ref, vis_ref, mod_ref, flag_ref, slot, tb):
+    same = (pm_ref[slot, 0] == pm_ref[slot, 1]).astype(F32)
+    at = slice(tb * 128, tb * 128 + 128)
+    base = iota((1, 128), 1) + tb * 128
+    diagonal = ((base >> 5) == (base & 31)).astype(F32)
+    weight = flag_ref[slot, :, at].astype(F32) * (1.0 - same * diagonal)
+    return [ref[c, slot, :, at].astype(F32) * weight for ref in (vis_ref, mod_ref) for c in range(2)]
+
+
+def channel_sums(pm_ref, vis_ref, mod_ref, flag_ref, pq_ref):
     for slot in range(2):
-        first = pm_ref[slot, 0]
-        second = pm_ref[slot, 1]
-        same = (first == second).astype(F32)
-        lane = iota((1, 128), 1)
-        planes = [[], [], [], []]
         for tb in range(8):
-            at = slice(tb * 128, tb * 128 + 128)
-            base = lane + tb * 128
-            diagonal = ((base >> 5) == (base & 31)).astype(F32)
-            weight = flag_ref[slot, :, at].astype(F32) * (1.0 - same * diagonal)
-            vr = vis_ref[0, slot, :, at].astype(F32) * weight
-            vi = vis_ref[1, slot, :, at].astype(F32) * weight
-            mr = mod_ref[0, slot, :, at].astype(F32) * weight
-            mi = mod_ref[1, slot, :, at].astype(F32) * weight
+            vr, vi, mr, mi = weighted(pm_ref, vis_ref, mod_ref, flag_ref, slot, tb)
             sums = (
                 jnp.sum(vr * mr + vi * mi, axis=0, keepdims=True),
                 jnp.sum(vi * mr - vr * mi, axis=0, keepdims=True),
@@ -54,15 +51,18 @@
             for q in range(3):
                 row = slot * 3 + q
                 pq_ref[tb // 2, row : row + 1, col] = sums[q]
-            for plane, value in zip(planes, (vr, vi, mr, mi)):
-                plane.append(value)
-        for q in range(4):
-            table = jnp.concatenate(planes[q], axis=0)
-            table_ref[q * 128 : q * 128 + 128, slot * 128 : slot * 128 + 128] = table.T.astype(BF16)
         for quarter in range(4):
             col = slice(slot * 128, slot * 128 + 128)
-            pq_ref[quarter, 6:7, col] = jnp.full((1, 128), first.astype(F32))
-            pq_ref[quarter, 7:8, col] = jnp.full((1, 128), second.astype(F32))
+            pq_ref[quarter, 6:7, col] = jnp.full((1, 128), pm_ref[slot, 0].astype(F32))
+            pq_ref[quarter, 7:8, col] = jnp.full((1, 128), pm_ref[slot, 1].astype(F32))
+
+
+def gather_tables(pm_ref, vis_ref, mod_ref, flag_ref, table_ref):
+    for slot in range(2):
+        planes = [weighted(pm_ref, vis_ref, mod_ref, flag_ref, slot, tb) for tb in range(8)]
+        for q in range(4):
+            table = jnp.concatenate([plane[q] for plane in planes], axis=0)
+            table_ref[q * 128 : q * 128 + 128, slot * 128 : slot * 128 + 128] = table.T.astype(BF16)
 
 
 def iota_table():
@@ -344,7 +344,7 @@
         remote(span, span, a2a_send.at[k], a2a_recv.at[k], {"chan_1": 1 - core}).wait()
         keep.wait()
 
-    sums_and_tables(pm_ref, vis_ref, mod_ref, flag_ref, pq_ref, table_ref)
+    channel_sums(pm_ref, vis_ref, mod_ref, flag_ref, pq_ref)
     pl.semaphore_wait(barrier, 16)
     for step in range(1, 4):
         signal(plane_sem, y_id(step))
@@ -355,6 +355,7 @@
 
     for step in range(1, 4):
         piece(step).start()
+    gather_tables(pm_ref, vis_ref, mod_ref, flag_ref, table_ref)
     iota_ref[...] = iota_table()
 
     def ints_step(group, carry):
@@ -382,9 +383,9 @@
         along(step).start()
     pl.semaphore_wait(plane_sem, 3)
     signal(far_sem, {"blk_0": 1 - xh})
+    gather(CUT[0], CUT[1])
     pl.semaphore_wait(far_sem, 1)
     keep_ints = to_owners(ints_ref, got_ints, 1)
-    gather(CUT[0], CUT[1])
 
     def line(k):
         count = (4, 3)[k]

time: 41 us -> 40.5 us (0.988)
    pallas_call x1, Pallas kernels: 38 us -> 37.6 us  [whole(): pl.pallas_call(kernel, name='whole', out_shape=(jax.ShapeDtypeStruct((2,...]
where the time goes in v5:
time: 40.5 us; the launch traced here: 40.4 us
  Pallas kernels  37.6 us (93%)
  local copies, waits for them, and re-layouts  2.17 us (5%)
  between operations  0.65 us (2%)
    pallas_call x1, Pallas kernels, whole(): pl.pallas_call(kernel, name='whole', out_shape=(jax.ShapeDtypeStruct((2,...  37.6 us
    unnamed x4, local copies, waits for them, and re-layouts  2.17 us

profile of v5, /device:TPU:1, one launch (start us, length us, event | category | flops | bytes accessed | tf_op | source)
XLA Modules:
  0.0 40.4 jit_solution(17093476141151121072)
XLA Ops:
  0.6 37.6 %whole.1 = (f32[2,128,128]{2,1,0:T(8,128)}, f32[2,512]{1,0:T(2,128)}) custom-call(s32[2,2]{1,0:T(2,128)} %pm_ref.1, bf16[2,2,16,1024]{3,2,1,0:T(8,128)(2,1)} %vis_ref.1, bf16[2,2,16,1024]{3,2,1,0:T(8,128)(2,1)} %mod_ref.1, s32[2,16,1024]{2,1,0:T(8,128)} %flag_ref.1, s32[64,256]{1,0:T(8,128)} %bitcast.7, s32[2,64,256]{2,1,0:T(8,128)} %bitcast.6, ...), custom_call_target="tpu_custom_call" | custom-call | tf_op jit(solution)/shard_map/whole/pallas_call | solution.py:502
  38.2 0.0 copy-start
  38.2 1.6 %copy.12 = f32[1,1,2,128,128]{4,3,2,1,0:T(8,128)} copy(f32[1,1,2,128,128]{4,3,2,1,0:T(8,128)} %bitcast.5) | data formatting | bytes 262144
  39.8 0.0 copy-done
  39.8 0.6 %copy.13 = f32[2,512]{1,0:T(2,128)} copy(f32[2,512]{1,0:T(2,128)S(1)} %copy-done) | data formatting | bytes 8192
Async XLA Ops:
  38.2 1.6 %copy-start = (f32[2,512]{1,0:T(2,128)S(1)}, f32[2,512]{1,0:T(2,128)}, u32[]{:S(2)}) copy-start(f32[2,512]{1,0:T(2,128)} %get-tuple-element.9) | copy-start | bytes 12292
